TPU v7x, 16 devices: a whole 2x2x2 slice. The times are simulated.
16 devices in a mesh: data: 2 (over z), group: 8 (over y, x, core).
Axes of the slice: x: 2, y: 2, z: 2, core: 2. Of those that a mesh axis runs over, the one named last changes fastest.
Arguments:
- latents: bfloat16 [2048, 1152], P(('data', 'group')), parts along dimension 0
- hint_embed: bfloat16 [2048, 1152], P(('data', 'group')), parts along dimension 0
- in_qkv: bfloat16 [2, 13, 1152, 3456], replicated
- in_proj: bfloat16 [2, 13, 16, 72, 1152], replicated
- in_up: bfloat16 [2, 13, 1152, 4608], replicated
- in_down: bfloat16 [2, 13, 4608, 1152], replicated
- in_norm: bfloat16 [2, 13, 4, 1152], replicated
- out_qkv: bfloat16 [12, 1152, 3456], replicated
- out_proj: bfloat16 [12, 16, 72, 1152], replicated
- out_up: bfloat16 [12, 1152, 4608], replicated
- out_down: bfloat16 [12, 4608, 1152], replicated
- out_norm: bfloat16 [12, 4, 1152], replicated
- zero_proj: bfloat16 [13, 1152, 1152], replicated
- hint_proj: bfloat16 [1152, 1152], replicated
- skip_proj: bfloat16 [12, 2304, 1152], replicated
- final_norm: bfloat16 [2, 1152], replicated
- w_out: bfloat16 [1152, 1152], replicated
Outputs:
- output: bfloat16 [2048, 1152], P(('data', 'group')), parts along dimension 0
There are 2 independent parts. A program takes and returns all parts, laid end to end along the dimension named above; an argument that names none is the same for every part.
All inputs are finite; a program needn't handle non-finite values.
Results may differ from a plain program's by a relative error of at most 0.02.
Values are sent between devices in bfloat16 or wider.
A program may use at most 5 GiB of HBM per device.

v0:
```python
import jax
import jax.numpy as jnp
from jax import lax
from jax.sharding import PartitionSpec as P

EPS = 1e-6


def mat_f32(left_op, right_op):
    return jnp.dot(left_op, right_op, preferred_element_type=jnp.float32)


def layer_norm(values, norm_gain, norm_shift):
    wide_vals = values.astype(jnp.float32)
    centered = wide_vals - jnp.mean(wide_vals, axis=-1, keepdims=True)
    variance = jnp.mean(centered * centered, axis=-1, keepdims=True)
    normed = centered * lax.rsqrt(variance + EPS)
    return (normed * norm_gain.astype(jnp.float32) + norm_shift.astype(jnp.float32)).astype(jnp.bfloat16)


def gather_half(local_rows, half_size):
    gathered = local_rows
    offset_bit = 1
    while offset_bit < half_size:
        partner_perm = [(dev_id, dev_id ^ offset_bit) for dev_id in range(2 * half_size)]
        gathered = jnp.concatenate([gathered, lax.ppermute(gathered, "group", partner_perm)], axis=0)
        offset_bit = offset_bit * 2
    return gathered


def transformer_block(residual, w_qkv, w_proj, w_up, w_down, norm_rows, half_size):
    tok_count, model_width = residual.shape
    head_count, head_dim = w_proj.shape[0], w_proj.shape[1]
    normed = layer_norm(residual, norm_rows[0], norm_rows[1])
    qkv_all = mat_f32(normed, w_qkv).astype(jnp.bfloat16)
    queries = qkv_all[:, :model_width].reshape(tok_count, head_count, head_dim)
    key_vals = gather_half(qkv_all[:, model_width:], half_size)
    key_heads = key_vals[:, :model_width].reshape(-1, head_count, head_dim)
    val_heads = key_vals[:, model_width:].reshape(-1, head_count, head_dim)
    scores = jnp.einsum("thd,nhd->htn", queries, key_heads, preferred_element_type=jnp.float32) * head_dim ** -0.5
    att_probs = jax.nn.softmax(scores, axis=-1).astype(jnp.bfloat16)
    head_out = jnp.einsum("htn,nhd->thd", att_probs, val_heads, preferred_element_type=jnp.float32).astype(jnp.bfloat16)
    attn_sum = jnp.einsum("thd,hde->te", head_out, w_proj, preferred_element_type=jnp.float32)
    residual = (residual.astype(jnp.float32) + attn_sum).astype(jnp.bfloat16)
    normed = layer_norm(residual, norm_rows[2], norm_rows[3])
    hidden = jax.nn.gelu(mat_f32(normed, w_up), approximate=True).astype(jnp.bfloat16)
    return (residual.astype(jnp.float32) + mat_f32(hidden, w_down)).astype(jnp.bfloat16)


def solution(mesh):
    group_size = mesh.shape["group"]
    half_size = group_size // 2
    swap_perm = [(dev_id, (dev_id + half_size) % group_size) for dev_id in range(group_size)]
    to_base = [(dev_id + half_size, dev_id) for dev_id in range(half_size)]
    to_ctrl = [(dev_id, dev_id + half_size) for dev_id in range(half_size)]

    def device_step(x_own, hint_own, in_qkv, in_proj, in_up, in_down, in_norm, out_qkv, out_proj, out_up, out_down, out_norm, zero_proj, hint_proj, skip_proj, final_norm, w_out):
        layers = skip_proj.shape[0]
        tok_own, model_width = x_own.shape
        branch = lax.axis_index("group") // half_size
        is_base = branch == 0
        x_other = lax.ppermute(x_own, "group", swap_perm)
        hint_recv = lax.ppermute(hint_own, "group", to_ctrl)
        x_local = jnp.where(is_base, jnp.concatenate([x_own, x_other], axis=0), jnp.concatenate([x_other, x_own], axis=0))
        hint_local = jnp.where(is_base, jnp.zeros((2 * tok_own, model_width), jnp.bfloat16), jnp.concatenate([hint_recv, hint_own], axis=0))
        residual = (x_local.astype(jnp.float32) + mat_f32(hint_local, hint_proj)).astype(jnp.bfloat16)
        sum_list = []
        for layer_idx in range(layers + 1):
            residual = transformer_block(residual, in_qkv[branch, layer_idx], in_proj[branch, layer_idx], in_up[branch, layer_idx], in_down[branch, layer_idx], in_norm[branch, layer_idx], half_size)
            ctrl_res = mat_f32(residual, zero_proj[layer_idx]).astype(jnp.bfloat16)
            res_recv = lax.ppermute(ctrl_res, "group", to_base)
            sum_list.append((residual.astype(jnp.float32) + res_recv.astype(jnp.float32)).astype(jnp.bfloat16))
        out_state = sum_list.pop()
        for layer_idx in range(layers):
            skip_val = sum_list[layers - 1 - layer_idx]
            top_part = mat_f32(out_state, skip_proj[layer_idx, :model_width])
            low_part = mat_f32(skip_val, skip_proj[layer_idx, model_width:])
            merged = (top_part + low_part).astype(jnp.bfloat16)
            out_state = transformer_block(merged, out_qkv[layer_idx], out_proj[layer_idx], out_up[layer_idx], out_down[layer_idx], out_norm[layer_idx], half_size)
        normed = layer_norm(out_state, final_norm[0], final_norm[1])
        y_local = mat_f32(normed, w_out).astype(jnp.bfloat16)
        y_recv = lax.ppermute(y_local[tok_own:], "group", to_ctrl)
        return jnp.where(is_base, y_local[:tok_own], y_recv)

    tok_spec = P(("data", "group"), None)
    return jax.shard_map(device_step, mesh=mesh, in_specs=(tok_spec, tok_spec) + (P(),) * 15, out_specs=tok_spec, check_vma=False)
```

profile of v0, /device:TPU:0, one launch (start us, length us, event | category | flops | bytes accessed | tf_op | source)
XLA Modules:
  0.0 2861.9 jit_solution(7765982239792129265)
XLA Ops:
  31.6 50.7 %collective-permute-done.3 = bf16[512,2304]{1,0:T(8,128)(2,1)} collective-permute-done((bf16[512,2304]{1,0:T(8,128)(2,1)}, bf16[512,2304]{1,0:T(8,128)(2,1)}, u32[]{:S(2)}, u32[]{:S(2)}) %collective-permute-start.3) | collective-permute-done | bytes 2359328 | tf_op jit(solution)/shard_map/ppermute | solution.py:26
  139.8 50.6 %collective-permute-done.5 = bf16[512,2304]{1,0:T(8,128)(2,1)} collective-permute-done((bf16[512,2304]{1,0:T(8,128)(2,1)}, bf16[512,2304]{1,0:T(8,128)(2,1)}, u32[]{:S(2)}, u32[]{:S(2)}) %collective-permute-start.5) | collective-permute-done | bytes 2359328 | tf_op jit(solution)/shard_map/ppermute | solution.py:26
  248.3 50.6 %collective-permute-done.7 = bf16[512,2304]{1,0:T(8,128)(2,1)} collective-permute-done((bf16[512,2304]{1,0:T(8,128)(2,1)}, bf16[512,2304]{1,0:T(8,128)(2,1)}, u32[]{:S(2)}, u32[]{:S(2)}) %collective-permute-start.7) | collective-permute-done | bytes 2359328 | tf_op jit(solution)/shard_map/ppermute | solution.py:26
  329.4 13.5 convert_reduce_fusion.9
  356.5 50.6 %collective-permute-done.9 = bf16[512,2304]{1,0:T(8,128)(2,1)} collective-permute-done((bf16[512,2304]{1,0:T(8,128)(2,1)}, bf16[512,2304]{1,0:T(8,128)(2,1)}, u32[]{:S(2)}, u32[]{:S(2)}) %collective-permute-start.9) | collective-permute-done | bytes 2359328 | tf_op jit(solution)/shard_map/ppermute | solution.py:26
  437.9 13.5 convert_reduce_fusion.8
  465.0 50.7 %collective-permute-done.11 = bf16[512,2304]{1,0:T(8,128)(2,1)} collective-permute-done((bf16[512,2304]{1,0:T(8,128)(2,1)}, bf16[512,2304]{1,0:T(8,128)(2,1)}, u32[]{:S(2)}, u32[]{:S(2)}) %collective-permute-start.11) | collective-permute-done | bytes 2359328 | tf_op jit(solution)/shard_map/ppermute | solution.py:26
  546.2 13.5 convert_reduce_fusion.7
  573.3 50.6 %collective-permute-done.13 = bf16[512,2304]{1,0:T(8,128)(2,1)} collective-permute-done((bf16[512,2304]{1,0:T(8,128)(2,1)}, bf16[512,2304]{1,0:T(8,128)(2,1)}, u32[]{:S(2)}, u32[]{:S(2)}) %collective-permute-start.13) | collective-permute-done | bytes 2359328 | tf_op jit(solution)/shard_map/ppermute | solution.py:26
  654.6 13.5 convert_reduce_fusion.6
  681.7 50.6 %collective-permute-done.15 = bf16[512,2304]{1,0:T(8,128)(2,1)} collective-permute-done((bf16[512,2304]{1,0:T(8,128)(2,1)}, bf16[512,2304]{1,0:T(8,128)(2,1)}, u32[]{:S(2)}, u32[]{:S(2)}) %collective-permute-start.15) | collective-permute-done | bytes 2359328 | tf_op jit(solution)/shard_map/ppermute | solution.py:26
  762.9 13.5 convert_reduce_fusion.5
  790.0 50.7 %collective-permute-done.17 = bf16[512,2304]{1,0:T(8,128)(2,1)} collective-permute-done((bf16[512,2304]{1,0:T(8,128)(2,1)}, bf16[512,2304]{1,0:T(8,128)(2,1)}, u32[]{:S(2)}, u32[]{:S(2)}) %collective-permute-start.17) | collective-permute-done | bytes 2359328 | tf_op jit(solution)/shard_map/ppermute | solution.py:26
  871.4 13.5 convert_reduce_fusion.4
  898.5 50.6 %collective-permute-done.19 = bf16[512,2304]{1,0:T(8,128)(2,1)} collective-permute-done((bf16[512,2304]{1,0:T(8,128)(2,1)}, bf16[512,2304]{1,0:T(8,128)(2,1)}, u32[]{:S(2)}, u32[]{:S(2)}) %collective-permute-start.19) | collective-permute-done | bytes 2359328 | tf_op jit(solution)/shard_map/ppermute | solution.py:26
  979.6 13.5 convert_reduce_fusion.3
  1006.7 50.6 %collective-permute-done.21 = bf16[512,2304]{1,0:T(8,128)(2,1)} collective-permute-done((bf16[512,2304]{1,0:T(8,128)(2,1)}, bf16[512,2304]{1,0:T(8,128)(2,1)}, u32[]{:S(2)}, u32[]{:S(2)}) %collective-permute-start.21) | collective-permute-done | bytes 2359328 | tf_op jit(solution)/shard_map/ppermute | solution.py:26
  1088.1 13.5 convert_reduce_fusion.2
  1115.3 50.6 %collective-permute-done.23 = bf16[512,2304]{1,0:T(8,128)(2,1)} collective-permute-done((bf16[512,2304]{1,0:T(8,128)(2,1)}, bf16[512,2304]{1,0:T(8,128)(2,1)}, u32[]{:S(2)}, u32[]{:S(2)}) %collective-permute-start.23) | collective-permute-done | bytes 2359328 | tf_op jit(solution)/shard_map/ppermute | solution.py:26
  1196.4 13.5 convert_reduce_fusion.1
  1223.5 50.6 %collective-permute-done.25 = bf16[512,2304]{1,0:T(8,128)(2,1)} collective-permute-done((bf16[512,2304]{1,0:T(8,128)(2,1)}, bf16[512,2304]{1,0:T(8,128)(2,1)}, u32[]{:S(2)}, u32[]{:S(2)}) %collective-permute-start.25) | collective-permute-done | bytes 2359328 | tf_op jit(solution)/shard_map/ppermute | solution.py:26
  1304.9 13.5 convert_reduce_fusion
  1337.1 45.5 %collective-permute-done.27 = bf16[512,2304]{1,0:T(8,128)(2,1)} collective-permute-done((bf16[512,2304]{1,0:T(8,128)(2,1)}, bf16[512,2304]{1,0:T(8,128)(2,1)}, u32[]{:S(2)}, u32[]{:S(2)}) %collective-permute-start.27) | collective-permute-done | bytes 2359328 | tf_op jit(solution)/shard_map/ppermute | solution.py:26
  1414.5 14.1 fusion.1162
  1470.2 45.7 %collective-permute-done.31 = bf16[512,2304]{1,0:T(8,128)(2,1)} collective-permute-done((bf16[512,2304]{1,0:T(8,128)(2,1)}, bf16[512,2304]{1,0:T(8,128)(2,1)}, u32[]{:S(2)}, u32[]{:S(2)}) %collective-permute-start.31) | collective-permute-done | bytes 2359328 | tf_op jit(solution)/shard_map/ppermute | solution.py:26
  1547.9 14.1 fusion.1341
  1587.0 45.8 %collective-permute-done.34 = bf16[512,2304]{1,0:T(8,128)(2,1)} collective-permute-done((bf16[512,2304]{1,0:T(8,128)(2,1)}, bf16[512,2304]{1,0:T(8,128)(2,1)}, u32[]{:S(2)}, u32[]{:S(2)}) %collective-permute-start.34) | collective-permute-done | bytes 2359328 | tf_op jit(solution)/shard_map/ppermute | solution.py:26
  1665.0 14.1 fusion.1338
  1704.8 45.0 %collective-permute-done.37 = bf16[512,2304]{1,0:T(8,128)(2,1)} collective-permute-done((bf16[512,2304]{1,0:T(8,128)(2,1)}, bf16[512,2304]{1,0:T(8,128)(2,1)}, u32[]{:S(2)}, u32[]{:S(2)}) %collective-permute-start.37) | collective-permute-done | bytes 2359328 | tf_op jit(solution)/shard_map/ppermute | solution.py:26
  1781.8 14.1 fusion.1335
  1820.9 45.8 %collective-permute-done.40 = bf16[512,2304]{1,0:T(8,128)(2,1)} collective-permute-done((bf16[512,2304]{1,0:T(8,128)(2,1)}, bf16[512,2304]{1,0:T(8,128)(2,1)}, u32[]{:S(2)}, u32[]{:S(2)}) %collective-permute-start.40) | collective-permute-done | bytes 2359328 | tf_op jit(solution)/shard_map/ppermute | solution.py:26
  1898.9 14.1 fusion.1332
  1937.9 45.8 %collective-permute-done.43 = bf16[512,2304]{1,0:T(8,128)(2,1)} collective-permute-done((bf16[512,2304]{1,0:T(8,128)(2,1)}, bf16[512,2304]{1,0:T(8,128)(2,1)}, u32[]{:S(2)}, u32[]{:S(2)}) %collective-permute-start.43) | collective-permute-done | bytes 2359328 | tf_op jit(solution)/shard_map/ppermute | solution.py:26
  2015.8 14.1 fusion.1329
  2054.8 45.8 %collective-permute-done.46 = bf16[512,2304]{1,0:T(8,128)(2,1)} collective-permute-done((bf16[512,2304]{1,0:T(8,128)(2,1)}, bf16[512,2304]{1,0:T(8,128)(2,1)}, u32[]{:S(2)}, u32[]{:S(2)}) %collective-permute-start.46) | collective-permute-done | bytes 2359328 | tf_op jit(solution)/shard_map/ppermute | solution.py:26
  2132.9 14.1 fusion.1326
  2172.7 45.0 %collective-permute-done.49 = bf16[512,2304]{1,0:T(8,128)(2,1)} collective-permute-done((bf16[512,2304]{1,0:T(8,128)(2,1)}, bf16[512,2304]{1,0:T(8,128)(2,1)}, u32[]{:S(2)}, u32[]{:S(2)}) %collective-permute-start.49) | collective-permute-done | bytes 2359328 | tf_op jit(solution)/shard_map/ppermute | solution.py:26
  2249.8 14.1 fusion.1323
  2288.9 45.7 %collective-permute-done.52 = bf16[512,2304]{1,0:T(8,128)(2,1)} collective-permute-done((bf16[512,2304]{1,0:T(8,128)(2,1)}, bf16[512,2304]{1,0:T(8,128)(2,1)}, u32[]{:S(2)}, u32[]{:S(2)}) %collective-permute-start.52) | collective-permute-done | bytes 2359328 | tf_op jit(solution)/shard_map/ppermute | solution.py:26
  2366.9 14.1 fusion.1320
  2406.0 45.7 %collective-permute-done.55 = bf16[512,2304]{1,0:T(8,128)(2,1)} collective-permute-done((bf16[512,2304]{1,0:T(8,128)(2,1)}, bf16[512,2304]{1,0:T(8,128)(2,1)}, u32[]{:S(2)}, u32[]{:S(2)}) %collective-permute-start.55) | collective-permute-done | bytes 2359328 | tf_op jit(solution)/shard_map/ppermute | solution.py:26
  2483.7 14.1 fusion.1317
  2522.8 45.8 %collective-permute-done.58 = bf16[512,2304]{1,0:T(8,128)(2,1)} collective-permute-done((bf16[512,2304]{1,0:T(8,128)(2,1)}, bf16[512,2304]{1,0:T(8,128)(2,1)}, u32[]{:S(2)}, u32[]{:S(2)}) %collective-permute-start.58) | collective-permute-done | bytes 2359328 | tf_op jit(solution)/shard_map/ppermute | solution.py:26
  2600.8 14.1 fusion.1314
  2639.9 45.8 %collective-permute-done.61 = bf16[512,2304]{1,0:T(8,128)(2,1)} collective-permute-done((bf16[512,2304]{1,0:T(8,128)(2,1)}, bf16[512,2304]{1,0:T(8,128)(2,1)}, u32[]{:S(2)}, u32[]{:S(2)}) %collective-permute-start.61) | collective-permute-done | bytes 2359328 | tf_op jit(solution)/shard_map/ppermute | solution.py:26
  2717.7 14.1 fusion.1311
  2752.0 50.6 %collective-permute-done.64 = bf16[512,2304]{1,0:T(8,128)(2,1)} collective-permute-done((bf16[512,2304]{1,0:T(8,128)(2,1)}, bf16[512,2304]{1,0:T(8,128)(2,1)}, u32[]{:S(2)}, u32[]{:S(2)}) %collective-permute-start.64) | collective-permute-done | bytes 2359328 | tf_op jit(solution)/shard_map/ppermute | solution.py:26
  2834.6 14.2 fusion.2458
  (897 shorter events, 1333.5 us)
Async XLA Ops:
  0.0 10.6 collective-permute-start
  3.3 12.6 collective-permute-start.1
  24.5 2.9 collective-permute-start.2
  28.9 53.3 %collective-permute-start.3 = (bf16[512,2304]{1,0:T(8,128)(2,1)}, bf16[512,2304]{1,0:T(8,128)(2,1)}, u32[]{:S(2)}, u32[]{:S(2)}) collective-permute-start(bf16[512,2304]{1,0:T(8,128)(2,1)} %pad_maximum_fusion.25), channel_id=1, source_target_pairs={{0,2},{1,3},{2,0},{3,1},{4,6},{5,7},{6,4},{7,5},{8,10},{9,11},{10,... | collective-permute-start | bytes 7077896 | tf_op jit(solution)/shard_map/ppermute | solution.py:26
  132.7 2.9 collective-permute-start.4
  137.2 53.3 %collective-permute-start.5 = (bf16[512,2304]{1,0:T(8,128)(2,1)}, bf16[512,2304]{1,0:T(8,128)(2,1)}, u32[]{:S(2)}, u32[]{:S(2)}) collective-permute-start(bf16[512,2304]{1,0:T(8,128)(2,1)} %pad_maximum_fusion.26), channel_id=1, source_target_pairs={{0,2},{1,3},{2,0},{3,1},{4,6},{5,7},{6,4},{7,5},{8,10},{9,11},{10,... | collective-permute-start | bytes 7077896 | tf_op jit(solution)/shard_map/ppermute | solution.py:26
  241.2 2.9 collective-permute-start.6
  245.7 53.3 %collective-permute-start.7 = (bf16[512,2304]{1,0:T(8,128)(2,1)}, bf16[512,2304]{1,0:T(8,128)(2,1)}, u32[]{:S(2)}, u32[]{:S(2)}) collective-permute-start(bf16[512,2304]{1,0:T(8,128)(2,1)} %pad_maximum_fusion.27), channel_id=1, source_target_pairs={{0,2},{1,3},{2,0},{3,1},{4,6},{5,7},{6,4},{7,5},{8,10},{9,11},{10,... | collective-permute-start | bytes 7077896 | tf_op jit(solution)/shard_map/ppermute | solution.py:26
  349.4 2.9 collective-permute-start.8
  353.9 53.3 %collective-permute-start.9 = (bf16[512,2304]{1,0:T(8,128)(2,1)}, bf16[512,2304]{1,0:T(8,128)(2,1)}, u32[]{:S(2)}, u32[]{:S(2)}) collective-permute-start(bf16[512,2304]{1,0:T(8,128)(2,1)} %pad_maximum_fusion.28), channel_id=1, source_target_pairs={{0,2},{1,3},{2,0},{3,1},{4,6},{5,7},{6,4},{7,5},{8,10},{9,11},{10,... | collective-permute-start | bytes 7077896 | tf_op jit(solution)/shard_map/ppermute | solution.py:26
  462.4 53.3 %collective-permute-start.11 = (bf16[512,2304]{1,0:T(8,128)(2,1)}, bf16[512,2304]{1,0:T(8,128)(2,1)}, u32[]{:S(2)}, u32[]{:S(2)}) collective-permute-start(bf16[512,2304]{1,0:T(8,128)(2,1)} %pad_maximum_fusion.29), channel_id=1, source_target_pairs={{0,2},{1,3},{2,0},{3,1},{4,6},{5,7},{6,4},{7,5},{8,10},{9,11},{10,... | collective-permute-start | bytes 7077896 | tf_op jit(solution)/shard_map/ppermute | solution.py:26
  570.6 53.3 %collective-permute-start.13 = (bf16[512,2304]{1,0:T(8,128)(2,1)}, bf16[512,2304]{1,0:T(8,128)(2,1)}, u32[]{:S(2)}, u32[]{:S(2)}) collective-permute-start(bf16[512,2304]{1,0:T(8,128)(2,1)} %pad_maximum_fusion.30), channel_id=1, source_target_pairs={{0,2},{1,3},{2,0},{3,1},{4,6},{5,7},{6,4},{7,5},{8,10},{9,11},{10,... | collective-permute-start | bytes 7077896 | tf_op jit(solution)/shard_map/ppermute | solution.py:26
  674.6 2.9 collective-permute-start.14
  679.1 53.3 %collective-permute-start.15 = (bf16[512,2304]{1,0:T(8,128)(2,1)}, bf16[512,2304]{1,0:T(8,128)(2,1)}, u32[]{:S(2)}, u32[]{:S(2)}) collective-permute-start(bf16[512,2304]{1,0:T(8,128)(2,1)} %pad_maximum_fusion.31), channel_id=1, source_target_pairs={{0,2},{1,3},{2,0},{3,1},{4,6},{5,7},{6,4},{7,5},{8,10},{9,11},{10,... | collective-permute-start | bytes 7077896 | tf_op jit(solution)/shard_map/ppermute | solution.py:26
  787.3 53.3 %collective-permute-start.17 = (bf16[512,2304]{1,0:T(8,128)(2,1)}, bf16[512,2304]{1,0:T(8,128)(2,1)}, u32[]{:S(2)}, u32[]{:S(2)}) collective-permute-start(bf16[512,2304]{1,0:T(8,128)(2,1)} %pad_maximum_fusion.32), channel_id=1, source_target_pairs={{0,2},{1,3},{2,0},{3,1},{4,6},{5,7},{6,4},{7,5},{8,10},{9,11},{10,... | collective-permute-start | bytes 7077896 | tf_op jit(solution)/shard_map/ppermute | solution.py:26
  895.8 53.3 %collective-permute-start.19 = (bf16[512,2304]{1,0:T(8,128)(2,1)}, bf16[512,2304]{1,0:T(8,128)(2,1)}, u32[]{:S(2)}, u32[]{:S(2)}) collective-permute-start(bf16[512,2304]{1,0:T(8,128)(2,1)} %pad_maximum_fusion.33), channel_id=1, source_target_pairs={{0,2},{1,3},{2,0},{3,1},{4,6},{5,7},{6,4},{7,5},{8,10},{9,11},{10,... | collective-permute-start | bytes 7077896 | tf_op jit(solution)/shard_map/ppermute | solution.py:26
  1004.0 53.3 %collective-permute-start.21 = (bf16[512,2304]{1,0:T(8,128)(2,1)}, bf16[512,2304]{1,0:T(8,128)(2,1)}, u32[]{:S(2)}, u32[]{:S(2)}) collective-permute-start(bf16[512,2304]{1,0:T(8,128)(2,1)} %pad_maximum_fusion.34), channel_id=1, source_target_pairs={{0,2},{1,3},{2,0},{3,1},{4,6},{5,7},{6,4},{7,5},{8,10},{9,11},{10,... | collective-permute-start | bytes 7077896 | tf_op jit(solution)/shard_map/ppermute | solution.py:26
  1112.6 53.3 %collective-permute-start.23 = (bf16[512,2304]{1,0:T(8,128)(2,1)}, bf16[512,2304]{1,0:T(8,128)(2,1)}, u32[]{:S(2)}, u32[]{:S(2)}) collective-permute-start(bf16[512,2304]{1,0:T(8,128)(2,1)} %pad_maximum_fusion.35), channel_id=1, source_target_pairs={{0,2},{1,3},{2,0},{3,1},{4,6},{5,7},{6,4},{7,5},{8,10},{9,11},{10,... | collective-permute-start | bytes 7077896 | tf_op jit(solution)/shard_map/ppermute | solution.py:26
  1220.9 53.3 %collective-permute-start.25 = (bf16[512,2304]{1,0:T(8,128)(2,1)}, bf16[512,2304]{1,0:T(8,128)(2,1)}, u32[]{:S(2)}, u32[]{:S(2)}) collective-permute-start(bf16[512,2304]{1,0:T(8,128)(2,1)} %pad_maximum_fusion.36), channel_id=1, source_target_pairs={{0,2},{1,3},{2,0},{3,1},{4,6},{5,7},{6,4},{7,5},{8,10},{9,11},{10,... | collective-permute-start | bytes 7077896 | tf_op jit(solution)/shard_map/ppermute | solution.py:26
  1329.3 53.3 %collective-permute-start.27 = (bf16[512,2304]{1,0:T(8,128)(2,1)}, bf16[512,2304]{1,0:T(8,128)(2,1)}, u32[]{:S(2)}, u32[]{:S(2)}) collective-permute-start(bf16[512,2304]{1,0:T(8,128)(2,1)} %pad_maximum_fusion.37), channel_id=1, source_target_pairs={{0,2},{1,3},{2,0},{3,1},{4,6},{5,7},{6,4},{7,5},{8,10},{9,11},{10,... | collective-permute-start | bytes 7077896 | tf_op jit(solution)/shard_map/ppermute | solution.py:26
  1335.8 97.7 %collective-permute-start.29 = (bf16[256,1152]{1,0:T(8,128)(2,1)}, bf16[256,1152]{1,0:T(8,128)(2,1)}, u32[]{:S(2)}, u32[]{:S(2)}) collective-permute-start(bf16[256,1152]{1,0:T(8,128)(2,1)} %fusion.1054), channel_id=1, source_target_pairs={{4,0},{5,1},{6,2},{7,3},{12,8},{13,9},{14,10},{15,11}} | collective-permute-start | bytes 1769480 | tf_op jit(solution)/shard_map/ppermute | solution.py:71
  1431.6 16.6 collective-permute-start.28
  1462.7 53.3 %collective-permute-start.31 = (bf16[512,2304]{1,0:T(8,128)(2,1)}, bf16[512,2304]{1,0:T(8,128)(2,1)}, u32[]{:S(2)}, u32[]{:S(2)}) collective-permute-start(bf16[512,2304]{1,0:T(8,128)(2,1)} %pad_maximum_fusion.38), channel_id=1, source_target_pairs={{0,2},{1,3},{2,0},{3,1},{4,6},{5,7},{6,4},{7,5},{8,10},{9,11},{10,... | collective-permute-start | bytes 7077896 | tf_op jit(solution)/shard_map/ppermute | solution.py:26
  1467.8 97.1 %collective-permute-start.32 = (bf16[256,1152]{1,0:T(8,128)(2,1)}, bf16[256,1152]{1,0:T(8,128)(2,1)}, u32[]{:S(2)}, u32[]{:S(2)}) collective-permute-start(bf16[256,1152]{1,0:T(8,128)(2,1)} %fusion.1057), channel_id=1, source_target_pairs={{4,0},{5,1},{6,2},{7,3},{12,8},{13,9},{14,10},{15,11}} | collective-permute-start | bytes 1769480 | tf_op jit(solution)/shard_map/ppermute | solution.py:71
  1579.5 53.3 %collective-permute-start.34 = (bf16[512,2304]{1,0:T(8,128)(2,1)}, bf16[512,2304]{1,0:T(8,128)(2,1)}, u32[]{:S(2)}, u32[]{:S(2)}) collective-permute-start(bf16[512,2304]{1,0:T(8,128)(2,1)} %pad_maximum_fusion.39), channel_id=1, source_target_pairs={{0,2},{1,3},{2,0},{3,1},{4,6},{5,7},{6,4},{7,5},{8,10},{9,11},{10,... | collective-permute-start | bytes 7077896 | tf_op jit(solution)/shard_map/ppermute | solution.py:26
  1584.6 97.3 %collective-permute-start.35 = (bf16[256,1152]{1,0:T(8,128)(2,1)}, bf16[256,1152]{1,0:T(8,128)(2,1)}, u32[]{:S(2)}, u32[]{:S(2)}) collective-permute-start(bf16[256,1152]{1,0:T(8,128)(2,1)} %fusion.1060), channel_id=1, source_target_pairs={{4,0},{5,1},{6,2},{7,3},{12,8},{13,9},{14,10},{15,11}} | collective-permute-start | bytes 1769480 | tf_op jit(solution)/shard_map/ppermute | solution.py:71
  1696.5 53.3 %collective-permute-start.37 = (bf16[512,2304]{1,0:T(8,128)(2,1)}, bf16[512,2304]{1,0:T(8,128)(2,1)}, u32[]{:S(2)}, u32[]{:S(2)}) collective-permute-start(bf16[512,2304]{1,0:T(8,128)(2,1)} %pad_maximum_fusion.40), channel_id=1, source_target_pairs={{0,2},{1,3},{2,0},{3,1},{4,6},{5,7},{6,4},{7,5},{8,10},{9,11},{10,... | collective-permute-start | bytes 7077896 | tf_op jit(solution)/shard_map/ppermute | solution.py:26
  1702.4 96.4 %collective-permute-start.38 = (bf16[256,1152]{1,0:T(8,128)(2,1)}, bf16[256,1152]{1,0:T(8,128)(2,1)}, u32[]{:S(2)}, u32[]{:S(2)}) collective-permute-start(bf16[256,1152]{1,0:T(8,128)(2,1)} %fusion.1063), channel_id=1, source_target_pairs={{4,0},{5,1},{6,2},{7,3},{12,8},{13,9},{14,10},{15,11}} | collective-permute-start | bytes 1769480 | tf_op jit(solution)/shard_map/ppermute | solution.py:71
  1813.4 53.3 %collective-permute-start.40 = (bf16[512,2304]{1,0:T(8,128)(2,1)}, bf16[512,2304]{1,0:T(8,128)(2,1)}, u32[]{:S(2)}, u32[]{:S(2)}) collective-permute-start(bf16[512,2304]{1,0:T(8,128)(2,1)} %pad_maximum_fusion.41), channel_id=1, source_target_pairs={{0,2},{1,3},{2,0},{3,1},{4,6},{5,7},{6,4},{7,5},{8,10},{9,11},{10,... | collective-permute-start | bytes 7077896 | tf_op jit(solution)/shard_map/ppermute | solution.py:26
  1818.4 97.4 %collective-permute-start.41 = (bf16[256,1152]{1,0:T(8,128)(2,1)}, bf16[256,1152]{1,0:T(8,128)(2,1)}, u32[]{:S(2)}, u32[]{:S(2)}) collective-permute-start(bf16[256,1152]{1,0:T(8,128)(2,1)} %fusion.1066), channel_id=1, source_target_pairs={{4,0},{5,1},{6,2},{7,3},{12,8},{13,9},{14,10},{15,11}} | collective-permute-start | bytes 1769480 | tf_op jit(solution)/shard_map/ppermute | solution.py:71
  1930.4 53.3 %collective-permute-start.43 = (bf16[512,2304]{1,0:T(8,128)(2,1)}, bf16[512,2304]{1,0:T(8,128)(2,1)}, u32[]{:S(2)}, u32[]{:S(2)}) collective-permute-start(bf16[512,2304]{1,0:T(8,128)(2,1)} %pad_maximum_fusion.42), channel_id=1, source_target_pairs={{0,2},{1,3},{2,0},{3,1},{4,6},{5,7},{6,4},{7,5},{8,10},{9,11},{10,... | collective-permute-start | bytes 7077896 | tf_op jit(solution)/shard_map/ppermute | solution.py:26
  1935.5 97.2 %collective-permute-start.44 = (bf16[256,1152]{1,0:T(8,128)(2,1)}, bf16[256,1152]{1,0:T(8,128)(2,1)}, u32[]{:S(2)}, u32[]{:S(2)}) collective-permute-start(bf16[256,1152]{1,0:T(8,128)(2,1)} %fusion.1069), channel_id=1, source_target_pairs={{4,0},{5,1},{6,2},{7,3},{12,8},{13,9},{14,10},{15,11}} | collective-permute-start | bytes 1769480 | tf_op jit(solution)/shard_map/ppermute | solution.py:71
  2042.9 2.9 collective-permute-start.45
  2047.3 53.3 %collective-permute-start.46 = (bf16[512,2304]{1,0:T(8,128)(2,1)}, bf16[512,2304]{1,0:T(8,128)(2,1)}, u32[]{:S(2)}, u32[]{:S(2)}) collective-permute-start(bf16[512,2304]{1,0:T(8,128)(2,1)} %pad_maximum_fusion.43), channel_id=1, source_target_pairs={{0,2},{1,3},{2,0},{3,1},{4,6},{5,7},{6,4},{7,5},{8,10},{9,11},{10,... | collective-permute-start | bytes 7077896 | tf_op jit(solution)/shard_map/ppermute | solution.py:26
  2052.4 97.4 %collective-permute-start.47 = (bf16[256,1152]{1,0:T(8,128)(2,1)}, bf16[256,1152]{1,0:T(8,128)(2,1)}, u32[]{:S(2)}, u32[]{:S(2)}) collective-permute-start(bf16[256,1152]{1,0:T(8,128)(2,1)} %fusion.1072), channel_id=1, source_target_pairs={{4,0},{5,1},{6,2},{7,3},{12,8},{13,9},{14,10},{15,11}} | collective-permute-start | bytes 1769480 | tf_op jit(solution)/shard_map/ppermute | solution.py:71
  2164.5 53.3 %collective-permute-start.49 = (bf16[512,2304]{1,0:T(8,128)(2,1)}, bf16[512,2304]{1,0:T(8,128)(2,1)}, u32[]{:S(2)}, u32[]{:S(2)}) collective-permute-start(bf16[512,2304]{1,0:T(8,128)(2,1)} %pad_maximum_fusion.44), channel_id=1, source_target_pairs={{0,2},{1,3},{2,0},{3,1},{4,6},{5,7},{6,4},{7,5},{8,10},{9,11},{10,... | collective-permute-start | bytes 7077896 | tf_op jit(solution)/shard_map/ppermute | solution.py:26
  2170.3 96.4 %collective-permute-start.50 = (bf16[256,1152]{1,0:T(8,128)(2,1)}, bf16[256,1152]{1,0:T(8,128)(2,1)}, u32[]{:S(2)}, u32[]{:S(2)}) collective-permute-start(bf16[256,1152]{1,0:T(8,128)(2,1)} %fusion.1075), channel_id=1, source_target_pairs={{4,0},{5,1},{6,2},{7,3},{12,8},{13,9},{14,10},{15,11}} | collective-permute-start | bytes 1769480 | tf_op jit(solution)/shard_map/ppermute | solution.py:71
  2281.3 53.3 %collective-permute-start.52 = (bf16[512,2304]{1,0:T(8,128)(2,1)}, bf16[512,2304]{1,0:T(8,128)(2,1)}, u32[]{:S(2)}, u32[]{:S(2)}) collective-permute-start(bf16[512,2304]{1,0:T(8,128)(2,1)} %pad_maximum_fusion.45), channel_id=1, source_target_pairs={{0,2},{1,3},{2,0},{3,1},{4,6},{5,7},{6,4},{7,5},{8,10},{9,11},{10,... | collective-permute-start | bytes 7077896 | tf_op jit(solution)/shard_map/ppermute | solution.py:26
  2286.5 97.3 %collective-permute-start.53 = (bf16[256,1152]{1,0:T(8,128)(2,1)}, bf16[256,1152]{1,0:T(8,128)(2,1)}, u32[]{:S(2)}, u32[]{:S(2)}) collective-permute-start(bf16[256,1152]{1,0:T(8,128)(2,1)} %fusion.1078), channel_id=1, source_target_pairs={{4,0},{5,1},{6,2},{7,3},{12,8},{13,9},{14,10},{15,11}} | collective-permute-start | bytes 1769480 | tf_op jit(solution)/shard_map/ppermute | solution.py:71
  2398.4 53.3 %collective-permute-start.55 = (bf16[512,2304]{1,0:T(8,128)(2,1)}, bf16[512,2304]{1,0:T(8,128)(2,1)}, u32[]{:S(2)}, u32[]{:S(2)}) collective-permute-start(bf16[512,2304]{1,0:T(8,128)(2,1)} %pad_maximum_fusion.46), channel_id=1, source_target_pairs={{0,2},{1,3},{2,0},{3,1},{4,6},{5,7},{6,4},{7,5},{8,10},{9,11},{10,... | collective-permute-start | bytes 7077896 | tf_op jit(solution)/shard_map/ppermute | solution.py:26
  2403.5 97.1 %collective-permute-start.56 = (bf16[256,1152]{1,0:T(8,128)(2,1)}, bf16[256,1152]{1,0:T(8,128)(2,1)}, u32[]{:S(2)}, u32[]{:S(2)}) collective-permute-start(bf16[256,1152]{1,0:T(8,128)(2,1)} %fusion.1081), channel_id=1, source_target_pairs={{4,0},{5,1},{6,2},{7,3},{12,8},{13,9},{14,10},{15,11}} | collective-permute-start | bytes 1769480 | tf_op jit(solution)/shard_map/ppermute | solution.py:71
  2510.8 2.9 collective-permute-start.57
  2515.3 53.3 %collective-permute-start.58 = (bf16[512,2304]{1,0:T(8,128)(2,1)}, bf16[512,2304]{1,0:T(8,128)(2,1)}, u32[]{:S(2)}, u32[]{:S(2)}) collective-permute-start(bf16[512,2304]{1,0:T(8,128)(2,1)} %pad_maximum_fusion.47), channel_id=1, source_target_pairs={{0,2},{1,3},{2,0},{3,1},{4,6},{5,7},{6,4},{7,5},{8,10},{9,11},{10,... | collective-permute-start | bytes 7077896 | tf_op jit(solution)/shard_map/ppermute | solution.py:26
  2520.4 97.4 %collective-permute-start.59 = (bf16[256,1152]{1,0:T(8,128)(2,1)}, bf16[256,1152]{1,0:T(8,128)(2,1)}, u32[]{:S(2)}, u32[]{:S(2)}) collective-permute-start(bf16[256,1152]{1,0:T(8,128)(2,1)} %fusion.1084), channel_id=1, source_target_pairs={{4,0},{5,1},{6,2},{7,3},{12,8},{13,9},{14,10},{15,11}} | collective-permute-start | bytes 1769480 | tf_op jit(solution)/shard_map/ppermute | solution.py:71
  2632.4 53.3 %collective-permute-start.61 = (bf16[512,2304]{1,0:T(8,128)(2,1)}, bf16[512,2304]{1,0:T(8,128)(2,1)}, u32[]{:S(2)}, u32[]{:S(2)}) collective-permute-start(bf16[512,2304]{1,0:T(8,128)(2,1)} %pad_maximum_fusion.48), channel_id=1, source_target_pairs={{0,2},{1,3},{2,0},{3,1},{4,6},{5,7},{6,4},{7,5},{8,10},{9,11},{10,... | collective-permute-start | bytes 7077896 | tf_op jit(solution)/shard_map/ppermute | solution.py:26
  2637.5 97.2 %collective-permute-start.62 = (bf16[256,1152]{1,0:T(8,128)(2,1)}, bf16[256,1152]{1,0:T(8,128)(2,1)}, u32[]{:S(2)}, u32[]{:S(2)}) collective-permute-start(bf16[256,1152]{1,0:T(8,128)(2,1)} %fusion.1087), channel_id=1, source_target_pairs={{4,0},{5,1},{6,2},{7,3},{12,8},{13,9},{14,10},{15,11}} | collective-permute-start | bytes 1769480 | tf_op jit(solution)/shard_map/ppermute | solution.py:71
  2749.3 53.3 %collective-permute-start.64 = (bf16[512,2304]{1,0:T(8,128)(2,1)}, bf16[512,2304]{1,0:T(8,128)(2,1)}, u32[]{:S(2)}, u32[]{:S(2)}) collective-permute-start(bf16[512,2304]{1,0:T(8,128)(2,1)} %pad_maximum_fusion.49), channel_id=1, source_target_pairs={{0,2},{1,3},{2,0},{3,1},{4,6},{5,7},{6,4},{7,5},{8,10},{9,11},{10,... | collective-permute-start | bytes 7077896 | tf_op jit(solution)/shard_map/ppermute | solution.py:26
  2853.4 7.4 collective-permute-start.65
  (175 other events, 1281.5 us)
where the time goes:
time: 2880 us; the launch traced here: 2860 us
  waiting for transfers between devices  1300 us (45%)
  matrix products  1120 us (39%)
  local copies, waits for them, and re-layouts  255 us (9%)
  other arithmetic  123 us (4%)
  starting transfers between devices  62.5 us (2%)
    ppermute x50, waiting for transfers between devices, gather_half(): lax.ppermute(gathered, 'group', partner_perm)  1280 us
    dot_general x89, matrix products, mat_f32(): return jnp.dot(left_op, right_op, preferred_element_type=jnp.float32)  617 us
    sub x25, matrix products, transformer_block(): att_probs = jax.nn.softmax(scores, axis=-1).astype(jnp.bfloat16)  259 us
    dot_general x25, matrix products, transformer_block(): jnp.einsum('thd,hde->te', head_out, w_proj, preferred_element_type=jnp.fl...  240 us
    slice x50, local copies, waits for them, and re-layouts, transformer_block(): key_heads = key_vals[:, :model_width].reshape(-1, head_count, head_dim)  130 us
    concatenate x50, other arithmetic, gather_half(): jnp.concatenate([gathered, lax.ppermute(gathered, 'group', partner_perm)]...  87.3 us
    slice x25, local copies, waits for them, and re-layouts, transformer_block(): val_heads = key_vals[:, model_width:].reshape(-1, head_count, head_dim)  83.6 us
  transfers between devices with their start and end apart: 66, of which 54 were waited for; matrix products, arithmetic and copies ran while one was open for 23% of the time, Pallas kernels for 0%

commit v1 on v0

v1 whole, which is shorter than its diff:
```python
import functools
import math

import jax
import jax.numpy as jnp
from jax import lax
from jax.experimental import pallas as pl
from jax.experimental.pallas import tpu as pltpu
from jax.sharding import PartitionSpec as P

EPS = 1e-6
BF = jnp.bfloat16
F32 = jnp.float32
MESH = pl.DeviceIdType.MESH
HEADS_PER_STEP = 4
GELU_C = math.sqrt(2.0 / math.pi)


def mat_f32(left_op, right_op):
    return jnp.dot(left_op, right_op, preferred_element_type=F32)


def layer_norm(values, norm_gain, norm_shift):
    wide_vals = values.astype(F32)
    centered = wide_vals - jnp.mean(wide_vals, axis=-1, keepdims=True)
    variance = jnp.mean(centered * centered, axis=-1, keepdims=True)
    normed = centered * lax.rsqrt(variance + EPS)
    return (normed * norm_gain.astype(F32) + norm_shift.astype(F32)).astype(BF)


def col_tiles(width, tile):
    return [(c, min(c + tile, width)) for c in range(0, width, tile)]


def norm_rows_into(dst, src, gain, shift):
    rows = dst.shape[0]
    for r in range(0, rows, 64):
        dst[r:r + 64, :] = layer_norm(src[r:r + 64, :], gain, shift)


class Block:
    def __init__(self, me, refs, heads):
        self.me = me
        self.__dict__.update(refs)
        self.rows, self.width = self.u.shape
        self.heads = heads
        self.hd = self.width // heads
        self.u_tiles = col_tiles(self.width, 512)
        self.kv_tiles = col_tiles(2 * self.width, 768)

    def remote(self, src, dst, send, recv, flip):
        peer = self.me + flip - 2 * flip * lax.rem(lax.div(self.me, flip), 2)
        return pltpu.make_async_remote_copy(
            src_ref=src, dst_ref=dst, send_sem=send, recv_sem=recv,
            device_id={"group": peer}, device_id_type=MESH)

    def u_copy(self, slot, c):
        lo, hi = self.u_tiles[c]
        return self.remote(self.u.at[:, lo:hi], self.uc.at[slot, :, lo:hi],
                           self.u_send.at[c], self.u_recv.at[slot, c], 2)

    def kv_copy(self, slot, which, c):
        lo, hi = self.kv_tiles[c]
        return self.remote(self.kv.at[slot, 2 * which, :, lo:hi],
                           self.kv.at[slot, 2 * which + 1, :, lo:hi],
                           self.kv_send.at[which, c], self.kv_recv.at[slot, which, c], 1)

    def project_kv(self, slot, which):
        for c, (lo, hi) in enumerate(self.kv_tiles):
            w = self.wqkv[:, self.width + lo:self.width + hi]
            self.kv[slot, 2 * which, :, lo:hi] = mat_f32(self.t[...], w).astype(BF)
            self.kv_copy(slot, which, c).start()

    def attend(self, slot, part):
        rows, width, hd = self.rows, self.width, self.hd
        scale = hd ** -0.5 * math.log2(math.e)
        win = 256
        lane = lax.broadcasted_iota(jnp.int32, (1, win), 1)

        def one_head(h):
            first = h * hd
            base = pl.multiple_of(jnp.minimum(first // 128, (width - win) // 128) * 128, 128)
            off = first - base
            inside = jnp.logical_and(lane >= off, lane < off + hd)
            keep = jnp.where(inside, 1.0, 0.0).astype(F32)
            q = self.q[:, pl.ds(base, win)] * keep.astype(BF)
            k = self.kv[slot, 2 * part:2 * part + 2, :, pl.ds(base, win)].reshape(2 * rows, win)
            v_base = pl.multiple_of(width + base, 128)
            v = self.kv[slot, 2 * part:2 * part + 2, :, pl.ds(v_base, win)].reshape(2 * rows, win)
            s = lax.dot_general(q, k, (((1,), (1,)), ((), ())), preferred_element_type=F32)
            m = jnp.max(s, axis=-1, keepdims=True)
            e = jnp.exp2((s - m) * scale)
            l = jnp.sum(e, axis=-1, keepdims=True)
            o = mat_f32(e.astype(BF), v)
            here = jnp.broadcast_to(inside, (rows, win))
            old = self.o[:, pl.ds(base, win)]
            if part == 0:
                self.m[h] = jnp.broadcast_to(m, (rows, 128))
                self.l[h] = jnp.broadcast_to(l, (rows, 128))
                self.o[:, pl.ds(base, win)] = jnp.where(here, o, old)
            else:
                m0, l0 = self.m[h], self.l[h]
                m1 = jnp.broadcast_to(m, (rows, 128))
                l1 = jnp.broadcast_to(l, (rows, 128))
                top = jnp.maximum(m0, m1)
                a0 = jnp.exp2((m0 - top) * scale)
                a1 = jnp.exp2((m1 - top) * scale)
                inv = 1.0 / (l0 * a0 + l1 * a1)
                a0, a1 = a0 * inv, a1 * inv
                a0 = jnp.concatenate([a0, a0], axis=1)
                a1 = jnp.concatenate([a1, a1], axis=1)
                self.o[:, pl.ds(base, win)] = jnp.where(here, old * a0 + o * a1, old)

        def step(g, carry):
            for d in range(HEADS_PER_STEP):
                one_head(g * HEADS_PER_STEP + d)
            return carry

        lax.fori_loop(0, self.heads // HEADS_PER_STEP, step, 0)

    def weight(self, idx, layer):
        return pltpu.make_async_copy(self.w_src[idx](layer), self.w_dst[idx], self.w_sem.at[idx])

    def refill(self, idx, layer, count):
        @pl.when(layer + 1 < count)
        def _():
            self.weight(idx, layer + 1).start()

    def run(self, i, count, filler, before_out, after_tile, out):
        p = lax.rem(i, 2)
        self.weight(0, i).wait()
        g1, b1 = self.norms[i, 0:1, :], self.norms[i, 1:2, :]
        norm_rows_into(self.t, self.u, g1, b1)
        self.project_kv(p, 0)
        self.q[...] = mat_f32(self.t[...], self.wqkv[:, :self.width]).astype(BF)
        for c in range(len(self.kv_tiles)):
            self.kv_copy(p, 0, c).wait_recv()
        self.attend(p, 0)
        filler()
        for c in range(len(self.u_tiles)):
            self.u_copy(p, c).wait_recv()
        norm_rows_into(self.t, self.uc.at[p], g1, b1)
        self.project_kv(p, 1)
        self.refill(0, i, count)
        for c in range(len(self.kv_tiles)):
            self.kv_copy(p, 1, c).wait_recv()
        self.attend(p, 1)
        for which in range(2):
            for c in range(len(self.kv_tiles)):
                self.kv_copy(p, which, c).wait_send()
        self.weight(1, i).wait()
        self.t[...] = self.o[...].astype(BF)
        for lo, hi in col_tiles(self.width, 512):
            attn = mat_f32(self.t[...], self.wo[:, lo:hi])
            self.u2[:, lo:hi] = (self.u[:, lo:hi].astype(F32) + attn).astype(BF)
        self.refill(1, i, count)
        norm_rows_into(self.t, self.u2, self.norms[i, 2:3, :], self.norms[i, 3:4, :])
        self.weight(2, i).wait()
        for lo, hi in col_tiles(self.hid.shape[1], 768):
            x = mat_f32(self.t[...], self.w1[:, lo:hi])
            g = 0.5 * x * (1.0 + jnp.tanh(GELU_C * (x + 0.044715 * (x * x * x))))
            self.hid[:, lo:hi] = g.astype(BF)
        self.refill(2, i, count)
        self.weight(3, i).wait()
        before_out()
        for c, (lo, hi) in enumerate(self.u_tiles):
            mlp = mat_f32(self.hid[...], self.w2[:, lo:hi])
            out[:, lo:hi] = (self.u2[:, lo:hi].astype(F32) + mlp).astype(BF)
            after_tile(c)
        self.refill(3, i, count)


def barrier(me, flips):
    sem = pltpu.get_barrier_semaphore()
    for flip in flips:
        peer = me + flip - 2 * flip * lax.rem(lax.div(me, flip), 2)
        pl.semaphore_signal(sem, inc=1, device_id={"group": peer}, device_id_type=MESH)
    pl.semaphore_wait(sem, len(flips))


COMMON = ("u", "u2", "uc", "t", "q", "kv", "o", "m", "l", "hid", "wqkv", "wo", "w1", "w2", "w_sem", "u_send", "u_recv", "kv_send", "kv_recv")


def common_scratch(rows, width, hidden, heads):
    u_n = len(col_tiles(width, 512))
    kv_n = len(col_tiles(2 * width, 768))
    return [
        pltpu.VMEM((rows, width), BF),
        pltpu.VMEM((rows, width), BF),
        pltpu.VMEM((2, rows, width), BF),
        pltpu.VMEM((rows, width), BF),
        pltpu.VMEM((rows, width), BF),
        pltpu.VMEM((2, 4, rows, 2 * width), BF),
        pltpu.VMEM((rows, width), F32),
        pltpu.VMEM((heads, rows, 128), F32),
        pltpu.VMEM((heads, rows, 128), F32),
        pltpu.VMEM((rows, hidden), BF),
        pltpu.VMEM((width, 3 * width), BF),
        pltpu.VMEM((width, width), BF),
        pltpu.VMEM((width, hidden), BF),
        pltpu.VMEM((hidden, width), BF),
        pltpu.SemaphoreType.DMA((5,)),
        pltpu.SemaphoreType.DMA((u_n,)),
        pltpu.SemaphoreType.DMA((2, u_n)),
        pltpu.SemaphoreType.DMA((2, kv_n)),
        pltpu.SemaphoreType.DMA((2, 2, kv_n)),
    ]


def in_kernel(heads, count, u0, norms, qkv_h, wo_h, w1_h, w2_h, wz_h, a_all, r_all, *scratch):
    refs = dict(zip(COMMON, scratch[:len(COMMON)]))
    wz, rbuf, r_send, r_recv, a_sem = scratch[len(COMMON):]
    me = lax.axis_index("group")
    branch = lax.div(me, 4)
    blk = Block(me, refs, heads)
    blk.norms = norms
    blk.w_src = [lambda i: qkv_h.at[branch, i], lambda i: wo_h.at[branch, i], lambda i: w1_h.at[branch, i],
                 lambda i: w2_h.at[branch, i], lambda i: wz_h.at[i]]
    blk.w_dst = [blk.wqkv, blk.wo, blk.w1, blk.w2, wz]
    for idx in range(4):
        blk.weight(idx, 0).start()

    @pl.when(branch == 1)
    def _():
        blk.weight(4, 0).start()

    blk.u[...] = u0[...]
    barrier(me, (1, 2, 4))
    for c in range(len(blk.u_tiles)):
        blk.u_copy(0, c).start()

    def a_store(i):
        return pltpu.make_async_copy(blk.u, a_all.at[i], a_sem)

    def r_copy(j):
        par = lax.rem(j, 2)
        return pltpu.make_async_remote_copy(
            src_ref=rbuf.at[par], dst_ref=r_all.at[j], send_sem=r_send.at[par], recv_sem=r_recv.at[j],
            device_id={"group": lax.rem(me, 4)}, device_id_type=MESH)

    def make_r(j):
        @pl.when(j >= 2)
        def _():
            r_copy(j - 2).wait_send()

        blk.weight(4, j).wait()
        par = lax.rem(j, 2)
        for lo, hi in col_tiles(blk.width, 512):
            rbuf[par, :, lo:hi] = mat_f32(blk.u[...], wz[:, lo:hi]).astype(BF)
        r_copy(j).start()
        blk.refill(4, j, count)

    def layer(i, carry):
        def filler():
            @pl.when(jnp.logical_and(branch == 1, i >= 1))
            def _():
                make_r(i - 1)

        def before_out():
            for c in range(len(blk.u_tiles)):
                blk.u_copy(0, c).wait_send()

            @pl.when(i >= 1)
            def _():
                a_store(i - 1).wait()

        def after_tile(c):
            @pl.when(i + 1 < count)
            def _():
                blk.u_copy(1 - lax.rem(i, 2), c).start()

        blk.run(i, count, filler, before_out, after_tile, blk.u)
        a_store(i).start()
        return carry

    lax.fori_loop(0, count, layer, 0)

    @pl.when(branch == 1)
    def _():
        make_r(jnp.int32(count - 1))
        if count >= 2:
            r_copy(jnp.int32(count - 2)).wait_send()
        r_copy(jnp.int32(count - 1)).wait_send()

    @pl.when(branch == 0)
    def _():
        def take(j, carry):
            r_copy(j).wait_recv()
            return carry
        lax.fori_loop(0, count, take, 0)

    a_store(count - 1).wait()


def out_kernel(heads, count, a_all, r_all, norms, qkv_h, wo_h, w1_h, w2_h, ws_h, y, *scratch):
    refs = dict(zip(COMMON, scratch[:len(COMMON)]))
    ws, pair, sa, sr, s_sem = scratch[len(COMMON):]
    me = lax.axis_index("group")

    def skip_load(j):
        idx = count - j
        return (pltpu.make_async_copy(a_all.at[idx], sa, s_sem.at[0]),
                pltpu.make_async_copy(r_all.at[idx], sr, s_sem.at[1]))

    def run_all():
        blk = Block(me, refs, heads)
        width = blk.width
        blk.norms = norms
        blk.w_src = [lambda i: qkv_h.at[i], lambda i: wo_h.at[i], lambda i: w1_h.at[i], lambda i: w2_h.at[i],
                     lambda i: ws_h.at[i]]
        blk.w_dst = [blk.wqkv, blk.wo, blk.w1, blk.w2, ws]
        for idx in (4, 0, 1, 2, 3):
            blk.weight(idx, 0).start()
        for cp in skip_load(0):
            cp.start()
        barrier(me, (1, 2))
        for cp in skip_load(0):
            cp.wait()
        pair[:, :width] = (sa[...].astype(F32) + sr[...].astype(F32)).astype(BF)
        for cp in skip_load(1):
            cp.start()

        def layer(i, carry):
            for cp in skip_load(i + 1):
                cp.wait()
            pair[:, width:] = (sa[...].astype(F32) + sr[...].astype(F32)).astype(BF)

            @pl.when(i + 1 < count)
            def _():
                for cp in skip_load(i + 2):
                    cp.start()

            blk.weight(4, i).wait()
            for c, (lo, hi) in enumerate(blk.u_tiles):
                blk.u[:, lo:hi] = mat_f32(pair[...], ws[:, lo:hi]).astype(BF)
                blk.u_copy(lax.rem(i, 2), c).start()
            blk.refill(4, i, count)

            def before_out():
                for c in range(len(blk.u_tiles)):
                    blk.u_copy(0, c).wait_send()

            blk.run(i, count, lambda: None, before_out, lambda c: None, pair.at[:, :width])
            return carry

        lax.fori_loop(0, count, layer, 0)
        y[...] = pair[:, :width]

    pl.when(lax.div(me, 4) == 0)(run_all)


def any_spec():
    return pl.BlockSpec(memory_space=pl.ANY)


def vmem_spec():
    return pl.BlockSpec(memory_space=pltpu.VMEM)


def solution(mesh):
    group_size = mesh.shape["group"]
    half_size = group_size // 2
    swap_perm = [(dev_id, (dev_id + half_size) % group_size) for dev_id in range(group_size)]
    to_ctrl = [(dev_id, dev_id + half_size) for dev_id in range(half_size)]

    def device_step(x_own, hint_own, in_qkv, in_proj, in_up, in_down, in_norm, out_qkv, out_proj, out_up, out_down, out_norm, zero_proj, hint_proj, skip_proj, final_norm, w_out):
        n_in, n_out = zero_proj.shape[0], skip_proj.shape[0]
        tok_own, width = x_own.shape
        rows = 2 * tok_own
        hidden = in_up.shape[-1]
        heads = in_proj.shape[2]
        branch = lax.axis_index("group") // half_size
        is_base = branch == 0
        x_other = lax.ppermute(x_own, "group", swap_perm)
        hint_recv = lax.ppermute(hint_own, "group", to_ctrl)
        x_local = jnp.where(is_base, jnp.concatenate([x_own, x_other], axis=0), jnp.concatenate([x_other, x_own], axis=0))
        hint_local = jnp.where(is_base, jnp.zeros((rows, width), BF), jnp.concatenate([hint_recv, hint_own], axis=0))
        u0 = (x_local.astype(F32) + mat_f32(hint_local, hint_proj)).astype(BF)
        norms = lax.dynamic_index_in_dim(in_norm, branch, 0, keepdims=False).astype(F32)
        params = dict(vmem_limit_bytes=67_000_000, has_side_effects=True)
        a_all, r_all = pl.pallas_call(
            functools.partial(in_kernel, heads, n_in),
            name="in_phase",
            out_shape=[jax.ShapeDtypeStruct((n_in, rows, width), BF)] * 2,
            in_specs=[vmem_spec(), vmem_spec()] + [any_spec()] * 5,
            out_specs=[any_spec(), any_spec()],
            scratch_shapes=common_scratch(rows, width, hidden, heads) + [
                pltpu.VMEM((width, width), BF),
                pltpu.VMEM((2, rows, width), BF),
                pltpu.SemaphoreType.DMA((2,)),
                pltpu.SemaphoreType.DMA((n_in,)),
                pltpu.SemaphoreType.DMA,
            ],
            compiler_params=pltpu.CompilerParams(collective_id=0, **params),
        )(u0, norms, in_qkv, in_proj.reshape(2, n_in, width, width), in_up, in_down, zero_proj)
        o_n = pl.pallas_call(
            functools.partial(out_kernel, heads, n_out),
            name="out_phase",
            out_shape=jax.ShapeDtypeStruct((rows, width), BF),
            in_specs=[any_spec()] * 2 + [vmem_spec()] + [any_spec()] * 5,
            out_specs=vmem_spec(),
            scratch_shapes=common_scratch(rows, width, hidden, heads) + [
                pltpu.VMEM((2 * width, width), BF),
                pltpu.VMEM((rows, 2 * width), BF),
                pltpu.VMEM((rows, width), BF),
                pltpu.VMEM((rows, width), BF),
                pltpu.SemaphoreType.DMA((2,)),
            ],
            compiler_params=pltpu.CompilerParams(collective_id=1, **params),
        )(a_all, r_all, out_norm.astype(F32), out_qkv, out_proj.reshape(n_out, width, width), out_up, out_down, skip_proj)
        y_local = mat_f32(layer_norm(o_n, final_norm[0], final_norm[1]), w_out).astype(BF)
        y_recv = lax.ppermute(y_local[tok_own:], "group", to_ctrl)
        return jnp.where(is_base, y_local[:tok_own], y_recv)

    tok_spec = P(("data", "group"), None)
    return jax.shard_map(device_step, mesh=mesh, in_specs=(tok_spec, tok_spec) + (P(),) * 15, out_specs=tok_spec, check_vma=False)
```

time: 2880 us -> 861 us (0.30)
  waiting for transfers between devices: 1300 us -> 13.1 us
  matrix products: 1120 us -> 6.58 us
  Pallas kernels: 0 us -> 826 us
  local copies, waits for them, and re-layouts: 255 us -> 0.04 us
  other arithmetic: 123 us -> 8.02 us
  starting transfers between devices: 62.5 us -> 6.48 us
    ppermute x63 -> x0, waiting for transfers between devices: 1290 us -> none  [the longest x50 1280 us: gather_half(): lax.ppermute(gathered, 'group', partner_perm)]
    dot_general x114 -> x2, matrix products: 857 us -> 6.58 us  [mat_f32(): return jnp.dot(left_op, right_op, preferred_element_type=F32)]
    pallas_call x0 -> x2, Pallas kernels: none -> 826 us  [the longest x1 414 us: device_step(): pl.pallas_call(functools.partial(in_kernel, heads, n_in), name='in_phase'...]
    sub x25 -> x0, matrix products: 259 us -> none  [transformer_block(): att_probs = jax.nn.softmax(scores, axis=-1).astype(jnp.bfloat16)]
    slice x150 -> x0, local copies, waits for them, and re-layouts: 244 us -> none  [the longest x50 130 us: transformer_block(): key_heads = key_vals[:, :model_width].reshape(-1, head_count, head_dim)]
    concatenate x50 -> x0, other arithmetic: 87.3 us -> none  [gather_half(): jnp.concatenate([gathered, lax.ppermute(gathered, 'group', partner_perm)]...]
    ppermute x63 -> x0, starting transfers between devices: 55.6 us -> none  [the longest x50 38.6 us: gather_half(): lax.ppermute(gathered, 'group', partner_perm)]
    reduce_sum x51 -> x1, other arithmetic: 30.2 us -> 1.36 us  [layer_norm(): variance = jnp.mean(centered * centered, axis=-1, keepdims=True)]
  transfers between devices with their start and end apart: 66 -> 3, of which waited for: 54 -> 3; matrix products, arithmetic and copies ran while one was open for 23% -> 1% of each run, Pallas kernels for 0% -> 0%
where the time goes in v1:
time: 861 us
  Pallas kernels  826 us (96%)
  waiting for transfers between devices  13.1 us (2%)
    pallas_call x1, Pallas kernels, device_step(): pl.pallas_call(functools.partial(in_kernel, heads, n_in), name='in_phase'...  414 us
    pallas_call x1, Pallas kernels, device_step(): pl.pallas_call(functools.partial(out_kernel, heads, n_out), name='out_pha...  412 us
  transfers between devices with their start and end apart: 3, of which 3 were waited for; matrix products, arithmetic and copies ran while one was open for 1% of the time, Pallas kernels for 0%

profile of v1, /device:TPU:0, one launch (start us, length us, event | category | flops | bytes accessed | tf_op | source)
XLA Modules:
  0.0 860.5 jit_solution(15049828951200619894)
XLA Ops:
  0.0 3.3 collective-permute-start
  3.3 1.9 collective-permute-start.1
  5.2 1.6 convert_element_type.31.norms
  6.8 1.4 convert_reduce_fusion.2
  8.2 1.6 bitcast_convert_fusion.norms
  9.8 0.8 collective-permute-done
  10.6 5.2 collective-permute-done.1
  15.8 3.8 add_convert_fusion.u0
  19.6 414.2 %in_phase.1 = (bf16[13,256,1152]{2,1,0:T(8,128)(2,1)}, bf16[13,256,1152]{2,1,0:T(8,128)(2,1)}) custom-call(bf16[256,1152]{1,0:T(8,128)(2,1)} %add_convert_fusion.u0, f32[13,4,1152]{2,1,0:T(4,128)} %bitcast_convert_fusion.norms, bf16[2,13,1152,3456]{3,2,1,0:T(8,128)(2,1)} %qkv_h.2, bf16[2,13,1152,1152]{3,2,1,0:T(8,128)(2,1)} %bitcast.1.wo_h, ...), custom_call_target="tpu_custom_call" | custom-call | tf_op jit(solution)/shard_map/in_phase/pallas_call | solution.py:381
  433.8 411.9 %out_phase.1 = bf16[256,1152]{1,0:T(8,128)(2,1)} custom-call(bf16[13,256,1152]{2,1,0:T(8,128)(2,1)} %get-tuple-element.7.a_all, bf16[13,256,1152]{2,1,0:T(8,128)(2,1)} %get-tuple-element.8.r_all, f32[12,4,1152]{2,1,0:T(4,128)} %convert_element_type.31.norms, bf16[12,1152,3456]{2,1,0:T(8,128)(2,1)} %qkv_h.3, bf16[12,1152,1152]{2,1,0:T(8,128)(2,1)} %bitcast.7, ...), custom_call_target="tpu_custom_call" | custom-call | tf_op jit(solution)/shard_map/out_phase/pallas_call | solution.py:396
  845.8 0.0 copy-start
  845.8 0.0 copy-start.1
  845.8 0.0 copy-start.2
  845.8 1.3 convert_reduce_fusion
  847.1 1.4 fusion.2
  848.5 0.0 copy-done
  848.5 0.0 copy-done.1
  848.5 0.0 copy-done.2
  848.5 2.8 convolution_convert_fusion
  851.4 1.3 collective-permute-start.2
  852.7 7.1 collective-permute-done.2
  859.7 0.8 slice_select_fusion
  (3 shorter events, 0.0 us)
Async XLA Ops:
  0.0 10.6 %collective-permute-start = (bf16[128,1152]{1,0:T(8,128)(2,1)}, bf16[128,1152]{1,0:T(8,128)(2,1)S(1)}, u32[]{:S(2)}, u32[]{:S(2)}) collective-permute-start(bf16[128,1152]{1,0:T(8,128)(2,1)} %param.17), channel_id=1, source_target_pairs={{0,4},{1,5},{2,6},{3,7},{4,0},{5,1},{6,2},{7,3},{8,12},{9,13},{10,... | collective-permute-start | bytes 884744 | tf_op jit(solution)/shard_map/ppermute | solution.py:374
  3.3 12.6 %collective-permute-start.1 = (bf16[128,1152]{1,0:T(8,128)(2,1)}, bf16[128,1152]{1,0:T(8,128)(2,1)S(1)}, u32[]{:S(2)}, u32[]{:S(2)}) collective-permute-start(bf16[128,1152]{1,0:T(8,128)(2,1)} %param.18), channel_id=1, source_target_pairs={{0,4},{1,5},{2,6},{3,7},{8,12},{9,13},{10,14},{11,15}} | collective-permute-start | bytes 884744 | tf_op jit(solution)/shard_map/ppermute | solution.py:375
  845.8 2.7 copy-start
  845.8 2.7 copy-start.1
  845.8 2.7 copy-start.2
  851.4 8.4 collective-permute-start.2

commit v2 on v1

v2 whole, which is shorter than its diff:
```python
import functools
import math

import jax
import jax.numpy as jnp
from jax import lax
from jax.experimental import pallas as pl
from jax.experimental.pallas import tpu as pltpu
from jax.sharding import PartitionSpec as P

EPS = 1e-6
BF = jnp.bfloat16
F32 = jnp.float32
MESH = pl.DeviceIdType.MESH
HEADS_PER_STEP = 4
U_TILE = 512
KV_TILE = 768
GELU_C = math.sqrt(2.0 / math.pi)


def mat_f32(left_op, right_op):
    return jnp.dot(left_op, right_op, preferred_element_type=F32)


def layer_norm(values, norm_gain, norm_shift):
    wide_vals = values.astype(F32)
    centered = wide_vals - jnp.mean(wide_vals, axis=-1, keepdims=True)
    variance = jnp.mean(centered * centered, axis=-1, keepdims=True)
    normed = centered * lax.rsqrt(variance + EPS)
    return (normed * norm_gain.astype(F32) + norm_shift.astype(F32)).astype(BF)


def col_tiles(width, tile):
    return [(c, min(c + tile, width)) for c in range(0, width, tile)]


def norm_rows_into(dst, src, lo, rows, gain, shift):
    for r in range(0, rows, 32):
        at = pl.ds(pl.multiple_of(lo + r, 32), 32)
        dst[at, :] = layer_norm(src[at, :], gain, shift)


def flipped(me, flip):
    return me + flip - 2 * flip * lax.rem(lax.div(me, flip), 2)


class Block:
    def __init__(self, me, refs, heads):
        self.me = me
        self.__dict__.update(refs)
        self.rows, self.width = self.u.shape
        self.heads = heads
        self.hd = self.width // heads
        self.half = self.rows // 2
        self.u_tiles = col_tiles(self.width, U_TILE)
        self.kv_tiles = col_tiles(2 * self.width, KV_TILE)

    def group(self, g):
        return pl.ds(pl.multiple_of(g * self.half, self.half), self.half)

    def remote(self, src, dst, send, recv, flip):
        return pltpu.make_async_remote_copy(
            src_ref=src, dst_ref=dst, send_sem=send, recv_sem=recv,
            device_id={"group": flipped(self.me, flip)}, device_id_type=MESH)

    def u_copy(self, slot, g, c):
        (lo, hi), at = self.u_tiles[c], self.group(g)
        return self.remote(self.u.at[at, lo:hi], self.uc.at[slot, at, lo:hi],
                           self.u_send.at[g, c], self.u_recv.at[slot, g, c], 2)

    def kv_copy(self, slot, g, c):
        lo, hi = self.kv_tiles[c]
        part, at, sem = (0, pl.ds(0, self.rows), 0) if g is None else (2, self.group(g), 1 + g)
        return self.remote(self.kv.at[slot, part, at, lo:hi],
                           self.kv.at[slot, part + 1, at, lo:hi],
                           self.kv_send.at[sem, c], self.kv_recv.at[slot, sem, c], 1)

    def project_kv(self, slot, g):
        part, at = (0, pl.ds(0, self.rows)) if g is None else (2, self.group(g))
        for c, (lo, hi) in enumerate(self.kv_tiles):
            w = self.wqkv[:, self.width + lo:self.width + hi]
            self.kv[slot, part, at, lo:hi] = mat_f32(self.t[at, :], w).astype(BF)
            self.kv_copy(slot, g, c).start()

    def attend(self, slot, part, lo, hi):
        rows, width, hd = self.rows, self.width, self.hd
        scale = hd ** -0.5 * math.log2(math.e)
        win = 256
        lane = lax.broadcasted_iota(jnp.int32, (1, win), 1)

        def place(h):
            first = h * hd
            base = pl.multiple_of(jnp.minimum(first // 128, (width - win) // 128) * 128, 128)
            off = first - base
            return base, jnp.logical_and(lane >= off, lane < off + hd)

        def scores(h):
            base, inside = place(h)
            keep = jnp.where(inside, 1.0, 0.0).astype(F32)
            q = self.q[:, pl.ds(base, win)] * keep.astype(BF)
            k = self.kv[slot, 2 * part:2 * part + 2, :, pl.ds(base, win)].reshape(2 * rows, win)
            return lax.dot_general(q, k, (((1,), (1,)), ((), ())), preferred_element_type=F32)

        def finish(h, s):
            base, inside = place(h)
            v_base = pl.multiple_of(width + base, 128)
            v = self.kv[slot, 2 * part:2 * part + 2, :, pl.ds(v_base, win)].reshape(2 * rows, win)
            m = jnp.max(s, axis=-1, keepdims=True)
            e = jnp.exp2((s - m) * scale)
            l = jnp.sum(e, axis=-1, keepdims=True)
            o = mat_f32(e.astype(BF), v)
            here = jnp.broadcast_to(inside, (rows, win))
            old = self.o[:, pl.ds(base, win)]
            if part == 0:
                self.m[h] = jnp.broadcast_to(m, (rows, 128))
                self.l[h] = jnp.broadcast_to(l, (rows, 128))
                self.o[:, pl.ds(base, win)] = jnp.where(here, o, old)
            else:
                m0, l0 = self.m[h], self.l[h]
                m1 = jnp.broadcast_to(m, (rows, 128))
                l1 = jnp.broadcast_to(l, (rows, 128))
                top = jnp.maximum(m0, m1)
                a0 = jnp.exp2((m0 - top) * scale)
                a1 = jnp.exp2((m1 - top) * scale)
                inv = 1.0 / (l0 * a0 + l1 * a1)
                a0, a1 = a0 * inv, a1 * inv
                a0 = jnp.concatenate([a0, a0], axis=1)
                a1 = jnp.concatenate([a1, a1], axis=1)
                self.o[:, pl.ds(base, win)] = jnp.where(here, old * a0 + o * a1, old)

        def step(at, carry):
            h0 = at * HEADS_PER_STEP
            s = scores(h0)
            for d in range(HEADS_PER_STEP):
                nxt = scores(h0 + d + 1) if d + 1 < HEADS_PER_STEP else None
                finish(h0 + d, s)
                s = nxt
            return carry

        lax.fori_loop(lo, hi, step, 0)

    def weight(self, idx, layer):
        return pltpu.make_async_copy(self.w_src[idx](layer), self.w_dst[idx], self.w_sem.at[idx])

    def refill(self, idx, layer, count):
        @pl.when(layer + 1 < count)
        def _():
            self.weight(idx, layer + 1).start()

    def run(self, i, count, filler, before_out, put):
        p = lax.rem(i, 2)
        n = self.norm_of(i)
        g1, b1, g2, b2 = n[0:1, :], n[1:2, :], n[2:3, :], n[3:4, :]
        every_kv, every_u = range(len(self.kv_tiles)), range(len(self.u_tiles))
        self.weight(0, i).wait()
        norm_rows_into(self.t, self.u, 0, self.rows, g1, b1)
        self.project_kv(p, None)
        self.q[...] = mat_f32(self.t[...], self.wqkv[:, :self.width]).astype(BF)
        for c in every_kv:
            self.kv_copy(p, None, c).wait_recv()

        def gather(g, carry):
            steps = self.heads // HEADS_PER_STEP // 2
            self.attend(p, 0, g * steps, (g + 1) * steps)
            for c in every_u:
                self.u_copy(p, g, c).wait_recv()
            norm_rows_into(self.t, self.uc.at[p], g * self.half, self.half, g1, b1)
            self.project_kv(p, g)
            return carry

        lax.fori_loop(0, 2, gather, 0)
        self.refill(0, i, count)
        filler()
        for g in range(2):
            for c in every_kv:
                self.kv_copy(p, g, c).wait_recv()
        self.attend(p, 1, 0, self.heads // HEADS_PER_STEP)
        for g in (None, 0, 1):
            for c in every_kv:
                self.kv_copy(p, g, c).wait_send()
        for idx in (1, 2, 3):
            self.weight(idx, i).wait()
        before_out()

        def finish(g, carry):
            at = self.group(g)
            self.t[at, :] = self.o[at, :].astype(BF)
            for lo, hi in col_tiles(self.width, 512):
                attn = mat_f32(self.t[at, :], self.wo[:, lo:hi])
                self.u2[at, lo:hi] = (self.u[at, lo:hi].astype(F32) + attn).astype(BF)
            norm_rows_into(self.t, self.u2, g * self.half, self.half, g2, b2)
            for lo, hi in col_tiles(self.hid.shape[1], 768):
                x = mat_f32(self.t[at, :], self.w1[:, lo:hi])
                gl = 0.5 * x * (1.0 + jnp.tanh(GELU_C * (x + 0.044715 * (x * x * x))))
                self.hid[:, lo:hi] = gl.astype(BF)
            for c in every_u:
                self.u_copy(0, g, c).wait_send()
            for c, (lo, hi) in enumerate(self.u_tiles):
                mlp = mat_f32(self.hid[...], self.w2[:, lo:hi])
                put(g, c, (self.u2[at, lo:hi].astype(F32) + mlp).astype(BF))
            return carry

        lax.fori_loop(0, 2, finish, 0)
        for idx in (1, 2, 3):
            self.refill(idx, i, count)


def barrier(me, flips):
    sem = pltpu.get_barrier_semaphore()
    for flip in flips:
        pl.semaphore_signal(sem, inc=1, device_id={"group": flipped(me, flip)}, device_id_type=MESH)
    pl.semaphore_wait(sem, len(flips))


COMMON = ("u", "u2", "uc", "t", "q", "kv", "o", "m", "l", "hid", "wqkv", "wo", "w1", "w2", "w_sem", "u_send", "u_recv", "kv_send", "kv_recv")


def common_scratch(rows, width, hidden, heads):
    u_n = len(col_tiles(width, U_TILE))
    kv_n = len(col_tiles(2 * width, KV_TILE))
    return [
        pltpu.VMEM((rows, width), BF),
        pltpu.VMEM((rows, width), BF),
        pltpu.VMEM((2, rows, width), BF),
        pltpu.VMEM((rows, width), BF),
        pltpu.VMEM((rows, width), BF),
        pltpu.VMEM((2, 4, rows, 2 * width), BF),
        pltpu.VMEM((rows, width), F32),
        pltpu.VMEM((heads, rows, 128), F32),
        pltpu.VMEM((heads, rows, 128), F32),
        pltpu.VMEM((rows // 2, hidden), BF),
        pltpu.VMEM((width, 3 * width), BF),
        pltpu.VMEM((width, width), BF),
        pltpu.VMEM((width, hidden), BF),
        pltpu.VMEM((hidden, width), BF),
        pltpu.SemaphoreType.DMA((6,)),
        pltpu.SemaphoreType.DMA((2, u_n)),
        pltpu.SemaphoreType.DMA((2, 2, u_n)),
        pltpu.SemaphoreType.DMA((3, kv_n)),
        pltpu.SemaphoreType.DMA((2, 3, kv_n)),
    ]


def in_kernel(heads, count, x_own, h_own, norms, hp_h, qkv_h, wo_h, w1_h, w2_h, wz_h, a_all, r_all, *scratch):
    refs = dict(zip(COMMON, scratch[:len(COMMON)]))
    wz, rbuf, r_send, r_recv, a_sem, x_sem = scratch[len(COMMON):]
    me = lax.axis_index("group")
    branch = lax.div(me, 4)
    blk = Block(me, refs, heads)
    blk.norm_of = lambda i: norms[branch, i].astype(F32)
    blk.w_src = [lambda i: qkv_h.at[branch, i], lambda i: wo_h.at[branch, i], lambda i: w1_h.at[branch, i],
                 lambda i: w2_h.at[branch, i], lambda i: wz_h.at[i]]
    blk.w_dst = [blk.wqkv, blk.wo, blk.w1, blk.w2, wz]
    hint_w = pltpu.make_async_copy(hp_h, wz, blk.w_sem.at[5])
    hint_w.start()
    for idx in range(4):
        blk.weight(idx, 0).start()
    barrier(me, (1, 2, 4))
    own = x_own.shape[0]

    give = blk.remote(blk.u2.at[0:own, :], blk.u.at[pl.ds(pl.multiple_of(branch * own, own), own), :],
                      x_sem.at[0], x_sem.at[1], 4)
    hint_w.wait()
    mine = pl.ds(pl.multiple_of(branch * own, own), own)
    for lo, hi in col_tiles(blk.width, 512):
        x = x_own[:, lo:hi]
        ctrl = (x.astype(F32) + mat_f32(h_own[...], wz[:, lo:hi])).astype(BF)
        blk.t[0:own, lo:hi] = ctrl

    @pl.when(branch == 0)
    def _():
        blk.u2[0:own, :] = blk.t[0:own, :]
        blk.u[mine, :] = x_own[...]

    @pl.when(branch == 1)
    def _():
        blk.u2[0:own, :] = x_own[...]
        blk.u[mine, :] = blk.t[0:own, :]
        blk.weight(4, 0).start()

    give.start()
    give.wait()
    for g in range(2):
        for c in range(len(blk.u_tiles)):
            blk.u_copy(0, g, c).start()

    def a_store(i):
        return pltpu.make_async_copy(blk.u, a_all.at[i], a_sem)

    def r_copy(j):
        par = lax.rem(j, 2)
        return pltpu.make_async_remote_copy(
            src_ref=rbuf.at[par], dst_ref=r_all.at[j], send_sem=r_send.at[par], recv_sem=r_recv.at[j],
            device_id={"group": lax.rem(me, 4)}, device_id_type=MESH)

    def make_r(j):
        @pl.when(j >= 2)
        def _():
            r_copy(j - 2).wait_send()

        blk.weight(4, j).wait()
        par = lax.rem(j, 2)
        for lo, hi in col_tiles(blk.width, 512):
            rbuf[par, :, lo:hi] = mat_f32(blk.u[...], wz[:, lo:hi]).astype(BF)
        r_copy(j).start()
        blk.refill(4, j, count)

    def layer(i, carry):
        def filler():
            @pl.when(jnp.logical_and(branch == 1, i >= 1))
            def _():
                make_r(i - 1)

        def before_out():
            @pl.when(i >= 1)
            def _():
                a_store(i - 1).wait()

        def put(g, c, values):
            lo, hi = blk.u_tiles[c]
            blk.u[blk.group(g), lo:hi] = values

            @pl.when(i + 1 < count)
            def _():
                blk.u_copy(1 - lax.rem(i, 2), g, c).start()

        blk.run(i, count, filler, before_out, put)
        a_store(i).start()
        return carry

    lax.fori_loop(0, count, layer, 0)

    @pl.when(branch == 1)
    def _():
        make_r(jnp.int32(count - 1))
        if count >= 2:
            r_copy(jnp.int32(count - 2)).wait_send()
        r_copy(jnp.int32(count - 1)).wait_send()

    @pl.when(branch == 0)
    def _():
        def take(j, carry):
            r_copy(j).wait_recv()
            return carry
        lax.fori_loop(0, count, take, 0)

    a_store(count - 1).wait()


def out_kernel(heads, count, a_all, r_all, norms, fin, qkv_h, wo_h, w1_h, w2_h, ws_h, wf_h, y, *scratch):
    refs = dict(zip(COMMON, scratch[:len(COMMON)]))
    top, low_w, low, o16, sa, sr, s_sem, y_sem = scratch[len(COMMON):]
    me = lax.axis_index("group")
    branch = lax.div(me, 4)
    own = y.shape[0]
    blk = Block(me, refs, heads)
    width = blk.width
    give = blk.remote(blk.u2.at[own:2 * own, :], y, y_sem.at[0], y_sem.at[1], 4)
    blk.norm_of = lambda i: norms[i].astype(F32)
    blk.w_src = [lambda i: qkv_h.at[i], lambda i: wo_h.at[i], lambda i: w1_h.at[i], lambda i: w2_h.at[i],
                 lambda i: ws_h.at[i, 0:width, :], lambda i: ws_h.at[i, width:2 * width, :]]
    blk.w_dst = [blk.wqkv, blk.wo, blk.w1, blk.w2, top, low_w]
    last_w = pltpu.make_async_copy(wf_h, blk.wo, blk.w_sem.at[1])

    def skip_load(j):
        idx = count - j
        return (pltpu.make_async_copy(a_all.at[idx], sa, s_sem.at[0]),
                pltpu.make_async_copy(r_all.at[idx], sr, s_sem.at[1]))

    def skip_sum(dst):
        for r in range(0, blk.rows, 32):
            dst[r:r + 32, :] = (sa[r:r + 32, :].astype(F32) + sr[r:r + 32, :].astype(F32)).astype(BF)

    def make_low(j):
        for cp in skip_load(j + 1):
            cp.wait()
        skip_sum(blk.t)

        @pl.when(j + 1 < count)
        def _():
            for cp in skip_load(j + 2):
                cp.start()

        blk.weight(5, j).wait()
        for lo, hi in col_tiles(width, 512):
            low[:, lo:hi] = mat_f32(blk.t[...], low_w[:, lo:hi])
        blk.refill(5, j, count)

    def merge(g, slot):
        at = blk.group(g)
        for c, (lo, hi) in enumerate(blk.u_tiles):
            blk.u[at, lo:hi] = (low[at, lo:hi] + mat_f32(o16[at, :], top[:, lo:hi])).astype(BF)
            blk.u_copy(slot, g, c).start()

    def run_all():
        for idx in (5, 4, 0, 1, 2, 3):
            blk.weight(idx, 0).start()
        for cp in skip_load(0):
            cp.start()
        barrier(me, (1, 2, 4))
        for cp in skip_load(0):
            cp.wait()
        skip_sum(o16)
        for cp in skip_load(1):
            cp.start()
        make_low(0)
        blk.weight(4, 0).wait()
        lax.fori_loop(0, 2, lambda g, carry: merge(g, 0) or carry, 0)
        blk.refill(4, 0, count)

        def layer(i, carry):
            def filler():
                @pl.when(i + 1 < count)
                def _():
                    make_low(i + 1)

            def before_out():
                @pl.when(i + 1 < count)
                def _():
                    blk.weight(4, i + 1).wait()

            def put(g, c, values):
                lo, hi = blk.u_tiles[c]
                o16[blk.group(g), lo:hi] = values
                if c == len(blk.u_tiles) - 1:
                    @pl.when(i + 1 < count)
                    def _():
                        merge(g, 1 - lax.rem(i, 2))

            blk.run(i, count, filler, before_out, put)
            blk.refill(4, i + 1, count)
            return carry

        lax.fori_loop(0, count, layer, 0)
        last_w.start()
        norm_rows_into(blk.t, o16, 0, blk.rows, fin[0:1, :].astype(F32), fin[1:2, :].astype(F32))
        last_w.wait()
        for r0, r1 in ((own, 2 * own), (0, own)):
            for lo, hi in col_tiles(width, 512):
                blk.u2[r0:r1, lo:hi] = mat_f32(blk.t[r0:r1, :], blk.wo[:, lo:hi]).astype(BF)
            if r0 > 0:
                give.start()
        y[...] = blk.u2[0:own, :]
        give.wait_send()

    pl.when(branch == 0)(run_all)

    @pl.when(branch == 1)
    def _():
        barrier(me, (4,))
        give.wait_recv()


def any_spec():
    return pl.BlockSpec(memory_space=pl.ANY)


def vmem_spec():
    return pl.BlockSpec(memory_space=pltpu.VMEM)


def solution(mesh):
    def device_step(x_own, hint_own, in_qkv, in_proj, in_up, in_down, in_norm, out_qkv, out_proj, out_up, out_down, out_norm, zero_proj, hint_proj, skip_proj, final_norm, w_out):
        n_in, n_out = zero_proj.shape[0], skip_proj.shape[0]
        tok_own, width = x_own.shape
        rows = 2 * tok_own
        hidden = in_up.shape[-1]
        heads = in_proj.shape[2]
        params = dict(vmem_limit_bytes=67_000_000, has_side_effects=True)
        a_all, r_all = pl.pallas_call(
            functools.partial(in_kernel, heads, n_in),
            name="in_phase",
            out_shape=[jax.ShapeDtypeStruct((n_in, rows, width), BF)] * 2,
            in_specs=[vmem_spec()] * 3 + [any_spec()] * 6,
            out_specs=[any_spec(), any_spec()],
            scratch_shapes=common_scratch(rows, width, hidden, heads) + [
                pltpu.VMEM((width, width), BF),
                pltpu.VMEM((2, rows, width), BF),
                pltpu.SemaphoreType.DMA((2,)),
                pltpu.SemaphoreType.DMA((n_in,)),
                pltpu.SemaphoreType.DMA,
                pltpu.SemaphoreType.DMA((2,)),
            ],
            compiler_params=pltpu.CompilerParams(collective_id=0, **params),
        )(x_own, hint_own, in_norm, hint_proj, in_qkv, in_proj.reshape(2, n_in, width, width), in_up, in_down, zero_proj)
        return pl.pallas_call(
            functools.partial(out_kernel, heads, n_out),
            name="out_phase",
            out_shape=jax.ShapeDtypeStruct((tok_own, width), BF),
            in_specs=[any_spec()] * 2 + [vmem_spec()] * 2 + [any_spec()] * 6,
            out_specs=vmem_spec(),
            scratch_shapes=common_scratch(rows, width, hidden, heads) + [
                pltpu.VMEM((width, width), BF),
                pltpu.VMEM((width, width), BF),
                pltpu.VMEM((rows, width), F32),
                pltpu.VMEM((rows, width), BF),
                pltpu.VMEM((rows, width), BF),
                pltpu.VMEM((rows, width), BF),
                pltpu.SemaphoreType.DMA((2,)),
                pltpu.SemaphoreType.DMA((2,)),
            ],
            compiler_params=pltpu.CompilerParams(collective_id=1, **params),
        )(a_all, r_all, out_norm, final_norm, out_qkv, out_proj.reshape(n_out, width, width), out_up, out_down, skip_proj, w_out)

    tok_spec = P(("data", "group"), None)
    return jax.shard_map(device_step, mesh=mesh, in_specs=(tok_spec, tok_spec) + (P(),) * 15, out_specs=tok_spec, check_vma=False)
```

time: 861 us -> 769 us (0.89)
  Pallas kernels: 826 us -> 767 us
  waiting for transfers between devices: 13.1 us -> 0 us
    pallas_call x1, Pallas kernels: 412 us -> 374 us  [device_step(): pl.pallas_call(functools.partial(out_kernel, heads, n_out), name='out_pha...]
    pallas_call x1, Pallas kernels: 414 us -> 393 us  [device_step(): pl.pallas_call(functools.partial(in_kernel, heads, n_in), name='in_phase'...]
    ppermute x3 -> x0, waiting for transfers between devices: 13.1 us -> none  [the longest x1 7.07 us: device_step(): y_recv = lax.ppermute(y_local[tok_own:], 'group', to_ctrl)]
  transfers between devices with their start and end apart: 3 -> 0, of which waited for: 3 -> 0; matrix products, arithmetic and copies ran while one was open for 1% -> 0% of each run, Pallas kernels for 0% -> 0%
where the time goes in v2:
time: 769 us; the launch traced here: 768 us
  Pallas kernels  767 us (100%)
    pallas_call x1, Pallas kernels, device_step(): pl.pallas_call(functools.partial(in_kernel, heads, n_in), name='in_phase'...  393 us
    pallas_call x1, Pallas kernels, device_step(): pl.pallas_call(functools.partial(out_kernel, heads, n_out), name='out_pha...  374 us

profile of v2, /device:TPU:0, one launch (start us, length us, event | category | flops | bytes accessed | tf_op | source)
XLA Modules:
  0.0 768.3 jit_solution(8896501382011692039)
XLA Ops:
  0.0 393.0 %in_phase.1 = (bf16[13,256,1152]{2,1,0:T(8,128)(2,1)}, bf16[13,256,1152]{2,1,0:T(8,128)(2,1)}) custom-call(bf16[128,1152]{1,0:T(8,128)(2,1)} %x_own.1, bf16[128,1152]{1,0:T(8,128)(2,1)} %h_own.1, bf16[2,13,4,1152]{3,2,1,0:T(4,128)(2,1)} %norms.2, bf16[1152,1152]{1,0:T(8,128)(2,1)} %hp_h.1, bf16[2,13,1152,3456]{3,2,1,0:T(8,128)(2,1)} %qkv_h.2, ...), custom_call_target="tpu_custom_call" | custom-call | tf_op jit(solution)/shard_map/in_phase/pallas_call | solution.py:470
  393.0 373.7 %out_phase.1 = bf16[128,1152]{1,0:T(8,128)(2,1)} custom-call(bf16[13,256,1152]{2,1,0:T(8,128)(2,1)} %get-tuple-element.7.a_all, bf16[13,256,1152]{2,1,0:T(8,128)(2,1)} %get-tuple-element.8.r_all, bf16[12,4,1152]{2,1,0:T(4,128)(2,1)} %norms.3, bf16[2,1152]{1,0:T(2,128)(2,1)} %fin.1, bf16[12,1152,3456]{2,1,0:T(8,128)(2,1)} %qkv_h.3, ...), custom_call_target="tpu_custom_call" | custom-call | tf_op jit(solution)/shard_map/out_phase/pallas_call | solution.py:486
  766.6 1.7 copy.19

commit v3 on v2

--- a/solution.py
+++ b/solution.py
@@ -12,7 +12,7 @@
 BF = jnp.bfloat16
 F32 = jnp.float32
 MESH = pl.DeviceIdType.MESH
-HEADS_PER_STEP = 4
+HEADS_PER_STEP = 8
 U_TILE = 512
 KV_TILE = 768
 GELU_C = math.sqrt(2.0 / math.pi)
@@ -84,6 +84,8 @@
 
     def attend(self, slot, part, lo, hi):
         rows, width, hd = self.rows, self.width, self.hd
+        chip, at = (0, pl.ds(0, rows)) if part == 0 else (2, self.group(part - 1))
+        keys = 2 * at.size
         scale = hd ** -0.5 * math.log2(math.e)
         win = 256
         lane = lax.broadcasted_iota(jnp.int32, (1, win), 1)
@@ -98,15 +100,15 @@
             base, inside = place(h)
             keep = jnp.where(inside, 1.0, 0.0).astype(F32)
             q = self.q[:, pl.ds(base, win)] * keep.astype(BF)
-            k = self.kv[slot, 2 * part:2 * part + 2, :, pl.ds(base, win)].reshape(2 * rows, win)
+            k = self.kv[slot, chip:chip + 2, at, pl.ds(base, win)].reshape(keys, win)
             return lax.dot_general(q, k, (((1,), (1,)), ((), ())), preferred_element_type=F32)
 
         def finish(h, s):
             base, inside = place(h)
             v_base = pl.multiple_of(width + base, 128)
-            v = self.kv[slot, 2 * part:2 * part + 2, :, pl.ds(v_base, win)].reshape(2 * rows, win)
-            m = jnp.max(s, axis=-1, keepdims=True)
-            e = jnp.exp2((s - m) * scale)
+            v = self.kv[slot, chip:chip + 2, at, pl.ds(v_base, win)].reshape(keys, win)
+            m = jnp.max(s, axis=-1, keepdims=True) * scale
+            e = jnp.exp2(s * scale - m)
             l = jnp.sum(e, axis=-1, keepdims=True)
             o = mat_f32(e.astype(BF), v)
             here = jnp.broadcast_to(inside, (rows, win))
@@ -120,10 +122,14 @@
                 m1 = jnp.broadcast_to(m, (rows, 128))
                 l1 = jnp.broadcast_to(l, (rows, 128))
                 top = jnp.maximum(m0, m1)
-                a0 = jnp.exp2((m0 - top) * scale)
-                a1 = jnp.exp2((m1 - top) * scale)
-                inv = 1.0 / (l0 * a0 + l1 * a1)
-                a0, a1 = a0 * inv, a1 * inv
+                a0 = jnp.exp2(m0 - top)
+                a1 = jnp.exp2(m1 - top)
+                total = l0 * a0 + l1 * a1
+                if part == 1:
+                    self.m[h], self.l[h] = top, total
+                else:
+                    inv = 1.0 / total
+                    a0, a1 = a0 * inv, a1 * inv
                 a0 = jnp.concatenate([a0, a0], axis=1)
                 a1 = jnp.concatenate([a1, a1], axis=1)
                 self.o[:, pl.ds(base, win)] = jnp.where(here, old * a0 + o * a1, old)
@@ -162,6 +168,13 @@
         def gather(g, carry):
             steps = self.heads // HEADS_PER_STEP // 2
             self.attend(p, 0, g * steps, (g + 1) * steps)
+
+            @pl.when(g == 1)
+            def _():
+                for c in every_kv:
+                    self.kv_copy(p, 0, c).wait_recv()
+                self.attend(p, 1, 0, self.heads // HEADS_PER_STEP)
+
             for c in every_u:
                 self.u_copy(p, g, c).wait_recv()
             norm_rows_into(self.t, self.uc.at[p], g * self.half, self.half, g1, b1)
@@ -171,10 +184,9 @@
         lax.fori_loop(0, 2, gather, 0)
         self.refill(0, i, count)
         filler()
-        for g in range(2):
-            for c in every_kv:
-                self.kv_copy(p, g, c).wait_recv()
-        self.attend(p, 1, 0, self.heads // HEADS_PER_STEP)
+        for c in every_kv:
+            self.kv_copy(p, 1, c).wait_recv()
+        self.attend(p, 2, 0, self.heads // HEADS_PER_STEP)
         for g in (None, 0, 1):
             for c in every_kv:
                 self.kv_copy(p, g, c).wait_send()

time: 769 us -> 791 us (1.029)
  Pallas kernels: 767 us -> 789 us
    pallas_call x1, Pallas kernels: 393 us -> 405 us  [device_step(): pl.pallas_call(functools.partial(in_kernel, heads, n_in), name='in_phase'...]
    pallas_call x1, Pallas kernels: 374 us -> 384 us  [device_step(): pl.pallas_call(functools.partial(out_kernel, heads, n_out), name='out_pha...]
where the time goes in v3:
time: 791 us
  Pallas kernels  789 us (100%)
    pallas_call x1, Pallas kernels, device_step(): pl.pallas_call(functools.partial(in_kernel, heads, n_in), name='in_phase'...  405 us
    pallas_call x1, Pallas kernels, device_step(): pl.pallas_call(functools.partial(out_kernel, heads, n_out), name='out_pha...  384 us

profile of v3, /device:TPU:0, one launch (start us, length us, event | category | flops | bytes accessed | tf_op | source)
XLA Modules:
  0.0 790.9 jit_solution(15296812082381468191)
XLA Ops:
  0.0 405.1 %in_phase.1 = (bf16[13,256,1152]{2,1,0:T(8,128)(2,1)}, bf16[13,256,1152]{2,1,0:T(8,128)(2,1)}) custom-call(bf16[128,1152]{1,0:T(8,128)(2,1)} %x_own.1, bf16[128,1152]{1,0:T(8,128)(2,1)} %h_own.1, bf16[2,13,4,1152]{3,2,1,0:T(4,128)(2,1)} %norms.2, bf16[1152,1152]{1,0:T(8,128)(2,1)} %hp_h.1, bf16[2,13,1152,3456]{3,2,1,0:T(8,128)(2,1)} %qkv_h.2, ...), custom_call_target="tpu_custom_call" | custom-call | tf_op jit(solution)/shard_map/in_phase/pallas_call | solution.py:482
  405.1 384.1 %out_phase.1 = bf16[128,1152]{1,0:T(8,128)(2,1)} custom-call(bf16[13,256,1152]{2,1,0:T(8,128)(2,1)} %get-tuple-element.7.a_all, bf16[13,256,1152]{2,1,0:T(8,128)(2,1)} %get-tuple-element.8.r_all, bf16[12,4,1152]{2,1,0:T(4,128)(2,1)} %norms.3, bf16[2,1152]{1,0:T(2,128)(2,1)} %fin.1, bf16[12,1152,3456]{2,1,0:T(8,128)(2,1)} %qkv_h.3, ...), custom_call_target="tpu_custom_call" | custom-call | tf_op jit(solution)/shard_map/out_phase/pallas_call | solution.py:498
  789.2 1.7 copy.19
